TPU v7x, 16 devices: a whole 2x2x2 slice. The times are simulated.
16 devices in a mesh: dp: 4 (over z, y), sp: 4 (over x, core).
Axes of the slice: x: 2, y: 2, z: 2, core: 2. Of those that a mesh axis runs over, the one named last changes fastest.
Arguments:
- latents: bfloat16 [16, 4, 1024, 1408], P('dp', 'sp'), parts along dimension 0
- text_ctx: bfloat16 [16, 256, 1408], P('dp'), parts along dimension 0
- modulation: float32 [16, 6, 1408], P('dp'), parts along dimension 0
- pos_temporal: float32 [4, 1408], replicated
- w_qkv_spatial: bfloat16 [3, 16, 88, 1408], replicated
- w_out_spatial: bfloat16 [16, 88, 1408], replicated
- w_qkv_temporal: bfloat16 [3, 16, 88, 1408], replicated
- w_out_temporal: bfloat16 [16, 88, 1408], replicated
- w_query_cross: bfloat16 [16, 88, 1408], replicated
- w_kv_cross: bfloat16 [2, 16, 88, 1408], replicated
- w_out_cross: bfloat16 [16, 88, 1408], replicated
- w_mlp_in: bfloat16 [1408, 5632], replicated
- w_mlp_out: bfloat16 [5632, 1408], replicated
Outputs:
- output: bfloat16 [16, 4, 1024, 1408], P('dp', 'sp'), parts along dimension 0
There are 4 independent parts. A program takes and returns all parts, laid end to end along the dimension named above; an argument that names none is the same for every part.
All inputs are finite; a program needn't handle non-finite values.
Results may differ from a plain program's by a relative error of at most 0.014981.
Values are sent between devices in bfloat16 or wider.
A program may use at most 1 GiB of HBM per device.

v0:
```python
import jax
import jax.numpy as jnp
from jax import lax
from jax.sharding import PartitionSpec as P

LN_EPS = 1e-6


def layer_norm(acts_in):
    centered = acts_in - jnp.mean(acts_in, axis=-1, keepdims=True)
    return centered * lax.rsqrt(jnp.mean(centered * centered, axis=-1, keepdims=True) + LN_EPS)


def spatial_sublayer(latents, mod_rows, w_qkv, w_out):
    head_dim = w_out.shape[1]
    lat_f = latents.astype(jnp.float32)
    normed = (layer_norm(lat_f) * (1.0 + mod_rows[1]) + mod_rows[0]).astype(jnp.bfloat16)
    qkv_all = jnp.einsum('btsc,jhdc->jbtshd', normed, w_qkv, preferred_element_type=jnp.float32).astype(jnp.bfloat16)
    scores = jnp.einsum('btqhd,btkhd->bthqk', qkv_all[0], qkv_all[1], preferred_element_type=jnp.float32)
    attn_probs = jax.nn.softmax(scores * (head_dim ** -0.5), axis=-1).astype(jnp.bfloat16)
    mixed_out = jnp.einsum('bthqk,btkhd->btqhd', attn_probs, qkv_all[2], preferred_element_type=jnp.float32).astype(jnp.bfloat16)
    branch = jnp.einsum('btshd,hdc->btsc', mixed_out, w_out, preferred_element_type=jnp.float32)
    return (lat_f + mod_rows[2] * branch).astype(jnp.bfloat16)


def temporal_sublayer(hidden, pos_temporal, gate_row, w_qkv, w_out):
    head_dim = w_out.shape[1]
    hid_f = hidden.astype(jnp.float32)
    shifted = (hid_f + pos_temporal[None, :, None, :]).astype(jnp.bfloat16)
    qkv_all = jnp.einsum('btsc,jhdc->jbtshd', shifted, w_qkv, preferred_element_type=jnp.float32).astype(jnp.bfloat16)
    scores = jnp.einsum('bqshd,bkshd->bshqk', qkv_all[0], qkv_all[1], preferred_element_type=jnp.float32)
    attn_probs = jax.nn.softmax(scores * (head_dim ** -0.5), axis=-1).astype(jnp.bfloat16)
    mixed_out = jnp.einsum('bshqk,bkshd->bqshd', attn_probs, qkv_all[2], preferred_element_type=jnp.float32).astype(jnp.bfloat16)
    branch = jnp.einsum('btshd,hdc->btsc', mixed_out, w_out, preferred_element_type=jnp.float32)
    return (hid_f + gate_row * branch).astype(jnp.bfloat16)


def cross_mlp(hidden, ctx_kv, mod_rows, w_query_cross, w_out_cross, w_mlp_in, w_mlp_out):
    head_dim = w_out_cross.shape[1]
    hid_f = hidden.astype(jnp.float32)
    query_heads = jnp.einsum('btsc,hdc->btshd', hidden, w_query_cross, preferred_element_type=jnp.float32).astype(jnp.bfloat16)
    scores = jnp.einsum('btshd,blhd->bthsl', query_heads, ctx_kv[0], preferred_element_type=jnp.float32)
    attn_probs = jax.nn.softmax(scores * (head_dim ** -0.5), axis=-1).astype(jnp.bfloat16)
    mixed_out = jnp.einsum('bthsl,blhd->btshd', attn_probs, ctx_kv[1], preferred_element_type=jnp.float32).astype(jnp.bfloat16)
    after_cross = (hid_f + jnp.einsum('btshd,hdc->btsc', mixed_out, w_out_cross, preferred_element_type=jnp.float32)).astype(jnp.bfloat16)
    cross_f = after_cross.astype(jnp.float32)
    normed = (layer_norm(cross_f) * (1.0 + mod_rows[4]) + mod_rows[3]).astype(jnp.bfloat16)
    mlp_hidden = jax.nn.gelu(jnp.einsum('btsc,cf->btsf', normed, w_mlp_in, preferred_element_type=jnp.float32), approximate=True).astype(jnp.bfloat16)
    mlp_out = jnp.einsum('btsf,fc->btsc', mlp_hidden, w_mlp_out, preferred_element_type=jnp.float32)
    return (cross_f + mod_rows[5] * mlp_out).astype(jnp.bfloat16)


def solution(mesh):
    act_spec = P('dp', 'sp', None, None)
    row_spec = P('dp', None, None)
    rep_two = P(None, None)
    rep_three = P(None, None, None)
    rep_four = P(None, None, None, None)
    in_specs = (act_spec, row_spec, row_spec, rep_two, rep_four, rep_three, rep_four, rep_three, rep_three, rep_four, rep_three, rep_two, rep_two)

    def local_block(latents, text_ctx, modulation, pos_temporal, w_qkv_spatial, w_out_spatial, w_qkv_temporal, w_out_temporal, w_query_cross, w_kv_cross, w_out_cross, w_mlp_in, w_mlp_out):
        mod_rows = jnp.moveaxis(modulation, 1, 0)[:, :, None, None, :]
        after_spatial = spatial_sublayer(latents, mod_rows, w_qkv_spatial, w_out_spatial)
        by_patch = lax.all_to_all(after_spatial, 'sp', 2, 1, tiled=True)
        after_temporal = temporal_sublayer(by_patch, pos_temporal, mod_rows[2], w_qkv_temporal, w_out_temporal)
        by_frame = lax.all_to_all(after_temporal, 'sp', 1, 2, tiled=True)
        ctx_kv = jnp.einsum('blc,jhdc->jblhd', text_ctx, w_kv_cross, preferred_element_type=jnp.float32).astype(jnp.bfloat16)
        return cross_mlp(by_frame, ctx_kv, mod_rows, w_query_cross, w_out_cross, w_mlp_in, w_mlp_out)

    return jax.shard_map(local_block, mesh=mesh, in_specs=in_specs, out_specs=act_spec, check_vma=False)
```

profile of v0, /device:TPU:0, one launch (start us, length us, event | category | flops | bytes accessed | tf_op | source)
XLA Modules:
  0.0 1222.6 jit_solution(3801775455320158349)
XLA Ops:
  0.0 0.0 copy-start
  0.0 1.6 slice_bitcast_fusion.24
  1.6 5.9 convert_reduce_fusion.1
  7.5 7.4 fusion.35
  14.9 65.0 %convert_bitcast_fusion.1 = bf16[3,4,1,1024,16,88]{3,5,4,0,1,2:T(8,128)(2,1)} fusion(bf16[3,16,88,1408]{3,2,1,0:T(8,128)(2,1)} %param.17, bf16[4,1,1024,1408]{3,2,1,0:T(8,128)(2,1)} %param.13, f32[4,1408]{1,0:T(4,128)S(1)} %get-tuple-element.13, f32[4,1408]{1,0:T(4,128)S(1)} %get-tuple-element.14, f32[4,1024]{1,0:T(4,128)S(1)} %add_rsqrt_fusion.1, ...), kind=kOutput, calls=%fused_computation.25 | convolution fusion | flops 48772939776 | bytes 58109952 | tf_op jit(solution)/shard_map/btsc,jhdc->jbtshd/dot_general | solution.py:18
  80.0 99.3 %fusion.123 = (f32[4,16,1024]{2,1,0:T(8,128)S(1)}, f32[4,16,1024,1024]{2,3,1,0:T(8,128)}) fusion(bf16[3,4,1,1024,16,88]{3,5,4,0,1,2:T(8,128)(2,1)} %convert_bitcast_fusion.1), kind=kOutput, calls=%fused_computation.128 | convolution fusion | flops 12012487680 | bytes 291766272 | tf_op jit(solution)/shard_map/sub | solution.py:20
  179.3 0.0 copy-start.4
  179.3 87.8 %fusion.158 = bf16[4,1024,16,88]{1,3,2,0:T(8,128)(2,1)} fusion(f32[4,16,1024,1024]{2,3,1,0:T(8,128)} %get-tuple-element.17, f32[4,16,1024]{2,1,0:T(8,128)S(1)} %get-tuple-element.16, bf16[3,4,1,1024,16,88]{3,5,4,0,1,2:T(8,128)(2,1)} %convert_bitcast_fusion.1), kind=kOutput, calls=%fused_computation.79.clone.1 | convolution fusion | flops 11951144960 | bytes 291766272 | tf_op jit(solution)/shard_map/bthqk,btkhd->btqhd/dot_general | solution.py:21
  267.1 0.0 copy-done.4
  267.1 24.9 %fusion.41 = bf16[4,1,1024,1408]{3,2,0,1:T(8,128)(2,1)S(1)} fusion(bf16[4,1,1024,1408]{3,2,1,0:T(8,128)(2,1)} %param.13, f32[4,1408]{1,0:T(4,128)S(1)} %copy-done.4, bf16[16,88,1408]{2,1,0:T(8,128)(2,1)} %param.18, bf16[4,1024,16,88]{1,3,2,0:T(8,128)(2,1)} %fusion.158), kind=kOutput, calls=%fused_computation.56 | convolution fusion | flops 16263413760 | bytes 38590464 | tf_op jit(solution)/shard_map/btshd,hdc->btsc/dot_general | solution.py:22
  291.9 58.2 %copy.36 = bf16[4,1,1024,1408]{3,0,1,2:T(4,128)(2,1)S(1)} copy(bf16[4,1,1024,1408]{3,2,0,1:T(8,128)(2,1)S(1)} %fusion.41) | data formatting | bytes 23068672 | tf_op jit(solution)/shard_map/convert_element_type | solution.py:23
  350.1 131.1 %all_to_all.21 = bf16[4,1,1024,1408]{3,0,1,2:T(4,128)(2,1)S(1)} all-to-all(bf16[4,1,1024,1408]{3,0,1,2:T(4,128)(2,1)S(1)} %copy.36), channel_id=1, replica_groups=mesh['dp'=4,'sp'=4] {'sp'}, dimensions={2} | all-to-all | bytes 23068672 | tf_op jit(solution)/shard_map/all_to_all | solution.py:64
  481.2 0.0 copy-start.6
  481.2 5.9 copy.37
  487.2 0.0 copy-done.6
  487.2 62.3 %convert_bitcast_fusion = bf16[3,4,4,256,16,88]{3,5,4,0,2,1:T(8,128)(2,1)} fusion(bf16[3,16,88,1408]{3,2,1,0:T(8,128)(2,1)} %param.19, bf16[4,4,256,1408]{3,2,1,0:T(8,128)(2,1)} %bitcast.251, f32[4,1408]{1,0:T(4,128)S(1)} %copy-done.6), kind=kOutput, calls=%fused_computation.24 | convolution fusion | flops 48755638272 | bytes 58054656 | tf_op jit(solution)/shard_map/btsc,jhdc->jbtshd/dot_general | solution.py:30
  549.4 22.4 %slice_bitcast_fusion = (bf16[4,4,256,16,88]{2,4,3,1,0:T(8,128)(2,1)}, bf16[4,4,256,16,88]{2,4,3,1,0:T(8,128)(2,1)}, bf16[4,4,256,16,88]{2,4,3,1,0:T(8,128)(2,1)}) fusion(bf16[3,4,4,256,16,88]{3,5,4,0,2,1:T(8,128)(2,1)} %convert_bitcast_fusion), kind=kLoop, calls=%fused_computation.72 | loop fusion | bytes 69206016 | tf_op jit(solution)/shard_map/squeeze | solution.py:31
  571.9 27.0 %copy.38 = bf16[4,4,256,16,88]{4,1,3,2,0:T(4,128)(2,1)} copy(bf16[4,4,256,16,88]{2,4,3,1,0:T(8,128)(2,1)} %get-tuple-element.6) | data formatting | bytes 23068672 | tf_op jit(solution)/shard_map/squeeze | solution.py:31
  598.9 27.0 %copy.39 = bf16[4,4,256,16,88]{4,1,3,2,0:T(4,128)(2,1)} copy(bf16[4,4,256,16,88]{2,4,3,1,0:T(8,128)(2,1)} %get-tuple-element.5) | data formatting | bytes 23068672 | tf_op jit(solution)/shard_map/squeeze | solution.py:31
  625.9 27.0 %copy.40 = bf16[4,4,256,16,88]{4,1,3,2,0:T(4,128)(2,1)} copy(bf16[4,4,256,16,88]{2,4,3,1,0:T(8,128)(2,1)} %get-tuple-element.7) | data formatting | bytes 23068672 | tf_op jit(solution)/shard_map/squeeze | solution.py:33
  652.9 63.8 %fusion.124 = (f32[4,256,16,4]{3,2,1,0:T(8,128)}, f32[4,256,16,4,4]{3,4,2,1,0:T(4,128)}) fusion(bf16[4,4,256,16,88]{4,1,3,2,0:T(4,128)(2,1)} %copy.38, bf16[4,4,256,16,88]{4,1,3,2,0:T(4,128)(2,1)} %copy.39), kind=kOutput, calls=%fused_computation.129 | convolution fusion | flops 46923780 | bytes 24379392 | tf_op jit(solution)/shard_map/sub | solution.py:32
  716.7 0.0 copy-start.5
  716.7 31.1 %fusion.55 = bf16[4,4,256,16,88]{4,1,3,2,0:T(4,128)(2,1)} fusion(bf16[4,4,256,16,88]{4,1,3,2,0:T(4,128)(2,1)} %copy.40, f32[4,256,16,4,4]{3,4,2,1,0:T(4,128)} %get-tuple-element.19, f32[4,256,16,4]{3,2,1,0:T(8,128)} %get-tuple-element.18), kind=kOutput, calls=%fused_computation.67 | convolution fusion | flops 52428800 | bytes 24379392 | tf_op jit(solution)/shard_map/bshqk,bkshd->bqshd/dot_general | solution.py:33
  747.8 0.0 copy-done.5
  747.8 41.8 %fusion.40 = bf16[4,4,256,1408]{3,2,1,0:T(8,128)(2,1)S(1)} fusion(bf16[4,4,256,1408]{3,2,1,0:T(8,128)(2,1)} %bitcast.252, bf16[4,4,256,16,88]{4,1,3,2,0:T(4,128)(2,1)} %fusion.55, f32[4,1408]{1,0:T(4,128)S(1)} %copy-done.5, bf16[16,88,1408]{2,1,0:T(8,128)(2,1)} %param.20), kind=kOutput, calls=%fused_computation.55 | convolution fusion | flops 16263413760 | bytes 38590464 | tf_op jit(solution)/shard_map/btshd,hdc->btsc/dot_general | solution.py:34
  789.6 4.9 copy.43
  794.5 6.4 all-to-all-start.1
  800.9 0.0 copy-done
  800.9 11.6 convert_bitcast_fusion.2
  812.5 2.9 slice_bitcast_fusion.22
  815.4 112.0 %all-to-all-done.1 = bf16[4,4,256,1408]{3,2,0,1:T(8,128)(2,1)} async-done(((bf16[4,4,256,1408]{3,2,0,1:T(8,128)(2,1)}), bf16[4,4,256,1408]{3,2,0,1:T(8,128)(2,1)}, u32[]{:S(2)}, u32[]{:S(2)}) %all-to-all-start.1) | async-done | bytes 11534368 | tf_op jit(solution)/shard_map/all_to_all | solution.py:66
  927.4 9.9 copy.44
  937.3 37.2 %bitcast_reduce_fusion = (f32[4,16,1024]{2,1,0:T(8,128)S(1)}, f32[4,16,256,1024]{3,2,1,0:T(8,128)}) fusion(bf16[4,1024,1408,1]{2,1,3,0:T(8,128)(2,1)} %bitcast.253, bf16[16,88,1408]{2,1,0:T(8,128)(2,1)} %param.21, bf16[4,256,16,88]{1,3,0,2:T(8,128)(2,1)} %get-tuple-element.9), kind=kOutput, calls=%fused_computation.18 | convolution fusion | flops 19232391168 | bytes 85753856 | tf_op jit(solution)/shard_map/btshd,blhd->bthsl/dot_general | solution.py:42
  974.5 21.1 %fusion.17 = f32[4,16,1024]{2,1,0:T(8,128)S(1)} fusion(f32[4,16,256,1024]{3,2,1,0:T(8,128)} %get-tuple-element.21, f32[4,16,1024]{2,1,0:T(8,128)S(1)} %get-tuple-element.20), kind=kLoop, calls=%fused_computation.21 | loop fusion | flops 50266112 | bytes 67633152 | tf_op jit(solution)/shard_map/reduce_sum | solution.py:43
  995.6 0.0 copy-start.2
  995.6 0.0 copy-start.3
  995.7 41.8 %convert_reduce_fusion = (f32[4,1024]{1,0:T(4,128)S(1)}, bf16[4,1024,1408]{2,1,0:T(8,128)(2,1)}) fusion(bf16[16,88,1408]{2,1,0:T(8,128)(2,1)} %param.23, f32[4,16,1024]{2,1,0:T(8,128)S(1)} %fusion.17, f32[4,16,1024]{2,1,0:T(8,128)S(1)} %get-tuple-element.20, f32[4,16,256,1024]{3,2,1,0:T(8,128)} %get-tuple-element.21, ...), kind=kOutput, calls=%fused_computation.28 | convolution fusion | flops 19294842880 | bytes 97566720 | tf_op jit(solution)/shard_map/btshd,hdc->btsc/dot_general | solution.py:45
  1037.4 7.4 fusion.31
  1044.9 0.0 copy-done.2
  1044.9 0.0 copy-done.3
  1044.9 0.0 copy-start.1
  1044.9 95.8 %fusion.162 = bf16[4,1024,5632]{2,1,0:T(8,128)(2,1)} fusion(bf16[1408,5632]{1,0:T(8,128)(2,1)} %param.24, bf16[4,1024,1408]{2,1,0:T(8,128)(2,1)} %get-tuple-element.23, f32[4,1408]{1,0:T(4,128)S(1)} %copy-done.2, f32[4,1408]{1,0:T(4,128)S(1)} %copy-done.3, f32[4,1024]{1,0:T(4,128)S(1)} %add_rsqrt_fusion, ...), kind=kOutput, calls=%fused_computation.23.clone.clone.clone.clone.clone.clone.clone.1 | convolution fusion | flops 65203601408 | bytes 73609216 | tf_op jit(solution)/shard_map/btsc,cf->btsf/dot_general | solution.py:48
  1140.7 0.0 copy-done.1
  1140.7 81.7 %fusion.88 = bf16[4,1,1024,1408]{3,2,1,0:T(8,128)(2,1)} fusion(bf16[5632,1408]{1,0:T(8,128)(2,1)} %param.25, bf16[4,1024,1408]{2,1,0:T(8,128)(2,1)} %get-tuple-element.23, f32[4,1408]{1,0:T(4,128)S(1)} %copy-done.1, bf16[4,1024,5632]{2,1,0:T(8,128)(2,1)} %fusion.162), kind=kOutput, calls=%fused_computation.94 | convolution fusion | flops 64984449024 | bytes 85088256 | tf_op jit(solution)/shard_map/btsf,fc->btsc/dot_general | solution.py:49
  (4 shorter events, 0.0 us)
Async XLA Ops:
  0.0 800.9 %copy-start = (bf16[4,256,1408]{2,1,0:T(8,128)(2,1)S(1)}, bf16[4,256,1408]{2,1,0:T(8,128)(2,1)}, u32[]{:S(2)}) copy-start(bf16[4,256,1408]{2,1,0:T(8,128)(2,1)} %param.14) | copy-start | bytes 8650756
  179.3 87.8 %copy-start.4 = (f32[4,1408]{1,0:T(4,128)S(1)}, f32[4,1408]{1,0:T(4,128)}, u32[]{:S(2)}) copy-start(f32[4,1408]{1,0:T(4,128)} %get-tuple-element.15) | copy-start | bytes 67588
  481.2 5.9 copy-start.6
  716.7 31.1 %copy-start.5 = (f32[4,1408]{1,0:T(4,128)S(1)}, f32[4,1408]{1,0:T(4,128)}, u32[]{:S(2)}) copy-start(f32[4,1408]{1,0:T(4,128)} %get-tuple-element.15) | copy-start | bytes 67588
  794.5 132.9 %all-to-all-start.1 = ((bf16[4,4,256,1408]{3,2,0,1:T(8,128)(2,1)}), bf16[4,4,256,1408]{3,2,0,1:T(8,128)(2,1)}, u32[]{:S(2)}, u32[]{:S(2)}) async-start(bf16[4,4,256,1408]{3,2,0,1:T(8,128)(2,1)} %copy.43), calls=%async_computation.1 | async-start | bytes 23068672 | tf_op jit(solution)/shard_map/all_to_all | solution.py:66
  995.6 49.3 %copy-start.2 = (f32[4,1408]{1,0:T(4,128)S(1)}, f32[4,1408]{1,0:T(4,128)}, u32[]{:S(2)}) copy-start(f32[4,1408]{1,0:T(4,128)} %get-tuple-element.11) | copy-start | bytes 67588
  995.6 49.3 %copy-start.3 = (f32[4,1408]{1,0:T(4,128)S(1)}, f32[4,1408]{1,0:T(4,128)}, u32[]{:S(2)}) copy-start(f32[4,1408]{1,0:T(4,128)} %get-tuple-element.12) | copy-start | bytes 67588
  1044.9 95.8 %copy-start.1 = (f32[4,1408]{1,0:T(4,128)S(1)}, f32[4,1408]{1,0:T(4,128)}, u32[]{:S(2)}) copy-start(f32[4,1408]{1,0:T(4,128)} %get-tuple-element.10) | copy-start | bytes 67588
where the time goes:
time: 1230 us; the launch traced here: 1220 us
  matrix products  744 us (60%)
  local copies, waits for them, and re-layouts  185 us (15%)
  blocking collectives  131 us (11%)
  waiting for transfers between devices  112 us (9%)
  other arithmetic  43.5 us (4%)
    all_to_all x1, blocking collectives, local_block(): by_patch = lax.all_to_all(after_spatial, 'sp', 2, 1, tiled=True)  131 us
    all_to_all x1, waiting for transfers between devices, local_block(): by_frame = lax.all_to_all(after_temporal, 'sp', 1, 2, tiled=True)  112 us
    sub x1, matrix products, spatial_sublayer(): jax.nn.softmax(scores * head_dim ** (-0.5), axis=-1).astype(jnp.bfloat16)  99.3 us
    dot_general x1, matrix products, cross_mlp(): jnp.einsum('btsc,cf->btsf', normed, w_mlp_in, preferred_element_type=jnp....  95.8 us
    dot_general x1, matrix products, spatial_sublayer(): jnp.einsum('bthqk,btkhd->btqhd', attn_probs, qkv_all[2], preferred_elemen...  87.8 us
    dot_general x1, matrix products, cross_mlp(): jnp.einsum('btsf,fc->btsc', mlp_hidden, w_mlp_out, preferred_element_type...  81.7 us
    dot_general x1, matrix products, spatial_sublayer(): jnp.einsum('btsc,jhdc->jbtshd', normed, w_qkv, preferred_element_type=jnp...  65 us
    sub x1, matrix products, temporal_sublayer(): jax.nn.softmax(scores * head_dim ** (-0.5), axis=-1).astype(jnp.bfloat16)  63.8 us
  transfers between devices with their start and end apart: 1, of which 1 were waited for; matrix products, arithmetic and copies ran while one was open for 1% of the time, Pallas kernels for 0%

commit v1 on v0

v1 whole, which is shorter than its diff:
```python
import functools

import jax
import jax.numpy as jnp
from jax import lax
from jax.experimental import pallas as pl
from jax.experimental.pallas import tpu as pltpu
from jax.sharding import PartitionSpec as P

LN_EPS = 1e-6
LOG2E = 1.4426950408889634
VMEM_LIMIT = 60 * 1024 * 1024
NT = (((1,), (1,)), ((), ()))
TN = (((0,), (0,)), ((), ()))
F32 = jnp.float32
BF16 = jnp.bfloat16


def dot(lhs, rhs, dims=(((1,), (0,)), ((), ()))):
    return lax.dot_general(lhs, rhs, dims, preferred_element_type=F32)


def normed_rows(rows, shift, scale):
    rows = rows.astype(F32)
    centered = rows - jnp.mean(rows, axis=-1, keepdims=True)
    unit = centered * lax.rsqrt(jnp.mean(centered * centered, axis=-1, keepdims=True) + LN_EPS)
    return (unit * (1.0 + scale) + shift).astype(BF16)


def resident(shape):
    return pl.BlockSpec(shape, lambda *_: (0,) * len(shape), pipeline_mode=pl.Buffered(1))


def project_heads(w_ref, acts, q_s, k_s, v_s, heads, dim, chunk):
    tokens = acts.shape[0]
    group = w_ref.shape[1]

    def body(i, carry):
        cols = pl.ds(pl.multiple_of(i * chunk, chunk), chunk)
        part = acts[cols, :]
        q_t = dot(w_ref[0], part, NT).reshape(heads, dim, chunk)
        q_s[:, :dim, cols] = q_t.astype(BF16)
        v_t = dot(w_ref[2], part, NT).reshape(heads, dim, chunk)
        v_s[:, :, cols] = v_t.astype(BF16)
        k_t = dot(w_ref[1], part, NT)
        for h in range(heads):
            k_s[h, cols, :dim] = k_t[h * dim:(h + 1) * dim].T.astype(BF16)
        return carry

    lax.fori_loop(0, tokens // chunk, body, 0)


def attend_block(k, v_t, q_t, scale):
    s = dot(k, q_t)
    p = jnp.exp2((s - jnp.max(s, axis=0, keepdims=True)) * scale)
    total = jnp.sum(p, axis=0, keepdims=True)
    return dot(v_t, p.astype(BF16)) / total


def spatial_kernel(me_ref, x_ref, mod_ref, w_ref, wo_hbm, o0, o1, o2, o3, u_s, q_s, k_s, v_s, a_s, wo_s, sem, *, heads, dim):
    g = pl.program_id(0)
    tokens = x_ref.shape[0]
    quarter = tokens // 4
    wo_copy = pltpu.make_async_copy(wo_hbm, wo_s, sem)
    scale = dim ** -0.5 * LOG2E

    @pl.when(g == 0)
    def _():
        wo_copy.start()
        q_s[:, dim:, :] = jnp.zeros((heads, q_s.shape[1] - dim, tokens), BF16)
        k_s[:, :, dim:] = jnp.zeros((heads, tokens, k_s.shape[2] - dim), BF16)

        def ln(i, carry):
            rows = pl.ds(pl.multiple_of(i * 128, 128), 128)
            u_s[rows, :] = normed_rows(x_ref[rows, :], mod_ref[0:1, :], mod_ref[1:2, :])
            return carry

        lax.fori_loop(0, tokens // 128, ln, 0)

    project_heads(w_ref, u_s, q_s, k_s, v_s, heads, dim, 512)

    def pair(i, carry):
        rows = pl.ds(pl.multiple_of((g * heads + 2 * i) * dim, 2 * dim), 2 * dim)
        for c in range(4):
            cols = slice(c * quarter, (c + 1) * quarter)
            outs = [attend_block(k_s[2 * i + h], v_s[2 * i + h], q_s[2 * i + h, :, cols], scale) for h in range(2)]
            a_s[rows, cols] = jnp.concatenate(outs, axis=0).astype(BF16)
        return carry

    lax.fori_loop(0, heads // 2, pair, 0)

    @pl.when(g == pl.num_programs(0) - 1)
    def _():
        wo_copy.wait()
        for d, o_ref in enumerate((o0, o1, o2, o3)):
            rows = pl.ds(pl.multiple_of(jnp.bitwise_xor(me_ref[0], d) * quarter, quarter), quarter)
            branch = dot(a_s[:, rows], wo_s[...], TN)
            o_ref[...] = (x_ref[rows, :].astype(F32) + mod_ref[2:3, :] * branch).astype(BF16)


def temporal_kernel(me_ref, x0, x1, x2, x3, mod_ref, pos_ref, w_ref, wo_hbm, o0, o1, o2, o3, z_s, q_s, k_s, v_s, a_s, wo_s, sem, *, heads, dim):
    g = pl.program_id(0)
    quarter = x0.shape[0]
    frames = (x0, x1, x2, x3)
    wo_copy = pltpu.make_async_copy(wo_hbm, wo_s, sem)
    scale = dim ** -0.5 * LOG2E

    @pl.when(g == 0)
    def _():
        wo_copy.start()
        for d, x in enumerate(frames):
            pos = pos_ref[pl.ds(jnp.bitwise_xor(me_ref[0], d), 1), :]
            z_s[d * quarter:(d + 1) * quarter, :] = (x[...].astype(F32) + pos).astype(BF16)

    def proj(i, carry):
        cols = pl.ds(pl.multiple_of(i * 512, 512), 512)
        part = z_s[cols, :]
        for j, dst in enumerate((q_s, k_s, v_s)):
            dst[:, :, cols] = dot(w_ref[j], part, NT).reshape(heads, dim, 512).astype(BF16)
        return carry

    lax.fori_loop(0, z_s.shape[0] // 512, proj, 0)

    def attend(h, cols):
        outs = []
        q = q_s[h].astype(F32)
        k = k_s[h].astype(F32)
        v = v_s[h].astype(F32)
        part = lambda a, t: a[:, t * quarter + cols:t * quarter + cols + 128]
        for tq in range(4):
            s = [jnp.sum(part(q, tq) * part(k, tk), axis=0, keepdims=True) for tk in range(4)]
            top = jnp.maximum(jnp.maximum(s[0], s[1]), jnp.maximum(s[2], s[3]))
            p = [jnp.exp2((one - top) * scale) for one in s]
            inv = 1.0 / (p[0] + p[1] + p[2] + p[3])
            p = [(one * inv).astype(BF16).astype(F32) for one in p]
            outs.append(p[0] * part(v, 0) + p[1] * part(v, 1) + p[2] * part(v, 2) + p[3] * part(v, 3))
        return outs

    def pair(i, carry):
        rows = pl.ds(pl.multiple_of((g * heads + 2 * i) * dim, 2 * dim), 2 * dim)
        for cols in range(0, quarter, 128):
            first = attend(2 * i, cols)
            second = attend(2 * i + 1, cols)
            for t in range(4):
                a_s[rows, t * quarter + cols:t * quarter + cols + 128] = jnp.concatenate([first[t], second[t]], axis=0).astype(BF16)
        return carry

    lax.fori_loop(0, heads // 2, pair, 0)

    @pl.when(g == pl.num_programs(0) - 1)
    def _():
        wo_copy.wait()
        for d, (x, o_ref) in enumerate(zip(frames, (o0, o1, o2, o3))):
            branch = dot(a_s[:, d * quarter:(d + 1) * quarter], wo_s[...], TN)
            o_ref[...] = (x[...].astype(F32) + mod_ref[2:3, :] * branch).astype(BF16)


def text_kernel(t_ref, w_ref, k_ref, v_ref, *, heads, dim):
    tokens = t_ref.shape[0]
    k_t = dot(w_ref[0], t_ref[...], NT)
    v_ref[...] = dot(w_ref[1], t_ref[...], NT).reshape(heads, dim, tokens).astype(BF16)
    for h in range(heads):
        k_ref[h] = k_t[h * dim:(h + 1) * dim].T.astype(BF16)


def cross_mlp_kernel(me_ref, x0, x1, x2, x3, mod_ref, k_ref, v_ref, wq_hbm, wo_hbm, w_in, w_out, *rest, heads, dim):
    y_ref, q_s, a_s, h_s, u_s, acc_s, wq_s, wo_s, sems = rest[-9:]
    step = pl.program_id(0)
    quarter = x0.shape[0]
    tokens = 4 * quarter
    scale = dim ** -0.5 * LOG2E

    @pl.when(step == 0)
    def _():
        q_copy = pltpu.make_async_copy(wq_hbm, wq_s, sems.at[0])
        o_copy = pltpu.make_async_copy(wo_hbm, wo_s, sems.at[1])
        q_copy.start()
        o_copy.start()
        q_copy.wait()
        for d, x in enumerate((x0, x1, x2, x3)):
            cols = slice(d * quarter, (d + 1) * quarter)
            q_s[:, :, cols] = dot(wq_s[...], x[...], NT).reshape(heads, dim, quarter).astype(BF16)

        def pair(i, carry):
            rows = pl.ds(pl.multiple_of(2 * i * dim, 2 * dim), 2 * dim)
            for d in range(4):
                cols = slice(d * quarter, (d + 1) * quarter)
                outs = [attend_block(k_ref[2 * i + h], v_ref[2 * i + h], q_s[2 * i + h, :, cols], scale) for h in range(2)]
                a_s[rows, cols] = jnp.concatenate(outs, axis=0).astype(BF16)
            return carry

        lax.fori_loop(0, heads // 2, pair, 0)
        o_copy.wait()
        for d, x in enumerate((x0, x1, x2, x3)):
            rows = slice(d * quarter, (d + 1) * quarter)
            branch = dot(a_s[:, rows], wo_s[...], TN)
            after = (x[...].astype(F32) + branch).astype(BF16)
            h_s[rows, :] = after
            u_s[rows, :] = normed_rows(after, mod_ref[3:4, :], mod_ref[4:5, :])

    def mlp(i, carry):
        rows = pl.ds(pl.multiple_of(i * 256, 256), 256)
        hidden = jax.nn.gelu(dot(u_s[rows, :], w_in[...]), approximate=True).astype(BF16)
        part = dot(hidden, w_out[...])

        @pl.when(step == 0)
        def _():
            acc_s[rows, :] = part

        @pl.when(step > 0)
        def _():
            acc_s[rows, :] += part

        return carry

    lax.fori_loop(0, tokens // 256, mlp, 0)

    @pl.when(step == pl.num_programs(0) - 1)
    def _():
        for d in range(4):
            rows = slice(d * quarter, (d + 1) * quarter)
            dst = pl.ds(pl.multiple_of(jnp.bitwise_xor(me_ref[0], d) * quarter, quarter), quarter)
            y_ref[dst, :] = (h_s[rows, :].astype(F32) + mod_ref[5:6, :] * acc_s[rows, :]).astype(BF16)


def cost(flops, nbytes, exps=0):
    return pl.CostEstimate(flops=int(flops), bytes_accessed=int(nbytes), transcendentals=int(exps))


def params():
    return pltpu.CompilerParams(dimension_semantics=("arbitrary",), vmem_limit_bytes=VMEM_LIMIT)


def spatial(me, latents, modulation, w_qkv, w_out, v, heads):
    tokens, width = latents.shape[2:]
    dim = w_qkv.shape[2]
    total = w_qkv.shape[1] * dim
    group, quarter = heads * dim, tokens // 4
    steps = w_qkv.shape[1] // heads
    spec = pltpu.PrefetchScalarGridSpec(
        num_scalar_prefetch=1,
        grid=(steps,),
        in_specs=[
            pl.BlockSpec((None, None, tokens, width), lambda g, me: (v, 0, 0, 0), pipeline_mode=pl.Buffered(1)),
            pl.BlockSpec((None, 6, width), lambda g, me: (v, 0, 0), pipeline_mode=pl.Buffered(1)),
            pl.BlockSpec((3, group, width), lambda g, me: (0, g, 0)),
            pl.BlockSpec(memory_space=pl.ANY),
        ],
        out_specs=[resident((quarter, width))] * 4,
        scratch_shapes=[
            pltpu.VMEM((tokens, width), BF16),
            pltpu.VMEM((heads, 128, tokens), BF16),
            pltpu.VMEM((heads, tokens, 128), BF16),
            pltpu.VMEM((heads, dim, tokens), BF16),
            pltpu.VMEM((total, tokens), BF16),
            pltpu.VMEM((total, width), BF16),
            pltpu.SemaphoreType.DMA,
        ],
    )
    return pl.pallas_call(
        functools.partial(spatial_kernel, heads=heads, dim=dim),
        grid_spec=spec,
        out_shape=[jax.ShapeDtypeStruct((quarter, width), BF16)] * 4,
        compiler_params=params(),
        cost_estimate=cost(2 * tokens * width * 4 * total + 4 * tokens * tokens * total, 2 * (4 * total * width + 2 * tokens * width), tokens * tokens * 16),
        name="spatial",
    )(me, latents, modulation, w_qkv.reshape(3, total, width), w_out.reshape(total, width))


def temporal(me, frames, modulation, pos, w_qkv, w_out, v, heads):
    quarter, width = frames[0].shape
    tokens = 4 * quarter
    dim = w_qkv.shape[2]
    total = w_qkv.shape[1] * dim
    group = heads * dim
    steps = w_qkv.shape[1] // heads
    spec = pltpu.PrefetchScalarGridSpec(
        num_scalar_prefetch=1,
        grid=(steps,),
        in_specs=[resident((quarter, width))] * 4 + [
            pl.BlockSpec((None, 6, width), lambda g, me: (v, 0, 0), pipeline_mode=pl.Buffered(1)),
            resident(pos.shape),
            pl.BlockSpec((3, group, width), lambda g, me: (0, g, 0)),
            pl.BlockSpec(memory_space=pl.ANY),
        ],
        out_specs=[resident((quarter, width))] * 4,
        scratch_shapes=[
            pltpu.VMEM((tokens, width), BF16),
            pltpu.VMEM((heads, dim, tokens), BF16),
            pltpu.VMEM((heads, dim, tokens), BF16),
            pltpu.VMEM((heads, dim, tokens), BF16),
            pltpu.VMEM((total, tokens), BF16),
            pltpu.VMEM((total, width), BF16),
            pltpu.SemaphoreType.DMA,
        ],
    )
    return pl.pallas_call(
        functools.partial(temporal_kernel, heads=heads, dim=dim),
        grid_spec=spec,
        out_shape=[jax.ShapeDtypeStruct((quarter, width), BF16)] * 4,
        compiler_params=params(),
        cost_estimate=cost(2 * tokens * width * 4 * total, 2 * (4 * total * width + 2 * tokens * width)),
        name="temporal",
    )(me, *frames, modulation, pos, w_qkv.reshape(3, total, width), w_out.reshape(total, width))


def text_kv(text, w_kv, heads):
    videos, length, width = text.shape
    dim = w_kv.shape[2]
    count = w_kv.shape[1]
    total = count * dim
    tokens = videos * length
    return pl.pallas_call(
        functools.partial(text_kernel, heads=heads, dim=dim),
        grid=(count // heads,),
        in_specs=[resident((tokens, width)), pl.BlockSpec((2, heads * dim, width), lambda g: (0, g, 0))],
        out_specs=[pl.BlockSpec((heads, tokens, dim), lambda g: (g, 0, 0)), pl.BlockSpec((heads, dim, tokens), lambda g: (g, 0, 0))],
        out_shape=[jax.ShapeDtypeStruct((count, tokens, dim), BF16), jax.ShapeDtypeStruct((count, dim, tokens), BF16)],
        compiler_params=params(),
        cost_estimate=cost(4 * tokens * width * total, 2 * (2 * total * width + 3 * tokens * width)),
        name="text_kv",
    )(text.reshape(tokens, width), w_kv.reshape(2, total, width))


def cross_mlp(me, chunks, modulation, k, v_t, w_query, w_out_cross, w_in, w_out, v, y, videos):
    quarter, width = chunks[0].shape
    tokens = 4 * quarter
    heads, all_text, dim = k.shape
    text = all_text // videos
    total = heads * dim
    hidden = w_in.shape[1]
    tile = 512
    steps = hidden // tile
    in_specs = [resident((quarter, width))] * 4 + [
        pl.BlockSpec((None, 6, width), lambda s, me: (v, 0, 0), pipeline_mode=pl.Buffered(1)),
        pl.BlockSpec((heads, text, dim), lambda s, me: (0, v, 0), pipeline_mode=pl.Buffered(1)),
        pl.BlockSpec((heads, dim, text), lambda s, me: (0, 0, v), pipeline_mode=pl.Buffered(1)),
        pl.BlockSpec(memory_space=pl.ANY),
        pl.BlockSpec(memory_space=pl.ANY),
        pl.BlockSpec((width, tile), lambda s, me: (0, s)),
        pl.BlockSpec((tile, width), lambda s, me: (s, 0)),
    ]
    args = [me, *chunks, modulation, k, v_t, w_query.reshape(total, width), w_out_cross.reshape(total, width), w_in, w_out]
    aliases = {}
    if y is not None:
        in_specs.append(pl.BlockSpec(memory_space=pl.ANY))
        aliases = {len(args): 0}
        args.append(y)
    spec = pltpu.PrefetchScalarGridSpec(
        num_scalar_prefetch=1,
        grid=(steps,),
        in_specs=in_specs,
        out_specs=pl.BlockSpec((None, None, tokens, width), lambda s, me: (v, 0, 0, 0), pipeline_mode=pl.Buffered(1)),
        scratch_shapes=[
            pltpu.VMEM((heads, dim, tokens), BF16),
            pltpu.VMEM((total, tokens), BF16),
            pltpu.VMEM((tokens, width), BF16),
            pltpu.VMEM((tokens, width), BF16),
            pltpu.VMEM((tokens, width), F32),
            pltpu.VMEM((total, width), BF16),
            pltpu.VMEM((total, width), BF16),
            pltpu.SemaphoreType.DMA((2,)),
        ],
    )
    return pl.pallas_call(
        functools.partial(cross_mlp_kernel, heads=heads, dim=dim),
        grid_spec=spec,
        out_shape=jax.ShapeDtypeStruct((videos, 1, tokens, width), BF16),
        input_output_aliases=aliases,
        compiler_params=params(),
        cost_estimate=cost(4 * tokens * width * (hidden + total) + 4 * tokens * text * total, 4 * (width * hidden + total * width + tokens * width)),
        name="cross_mlp",
    )(*args)


def swap(parts, devices):
    return [parts[0]] + [lax.ppermute(parts[d], 'sp', [(i, i ^ d) for i in range(devices)]) for d in range(1, devices)]


def solution(mesh):
    act_spec = P('dp', 'sp', None, None)
    row_spec = P('dp', None, None)
    rep_two = P(None, None)
    rep_three = P(None, None, None)
    rep_four = P(None, None, None, None)
    in_specs = (act_spec, row_spec, row_spec, rep_two, rep_four, rep_three, rep_four, rep_three, rep_three, rep_four, rep_three, rep_two, rep_two)
    devices = mesh.shape['sp']

    def local_block(latents, text_ctx, modulation, pos_temporal, w_qkv_spatial, w_out_spatial, w_qkv_temporal, w_out_temporal, w_query_cross, w_kv_cross, w_out_cross, w_mlp_in, w_mlp_out):
        videos = latents.shape[0]
        me = lax.axis_index('sp').astype(jnp.int32).reshape(1)
        by_patch = [swap(spatial(me, latents, modulation, w_qkv_spatial, w_out_spatial, v, 4), devices) for v in range(videos)]
        k, v_t = text_kv(text_ctx, w_kv_cross, 4)
        by_frame = [swap(temporal(me, by_patch[v], modulation, pos_temporal, w_qkv_temporal, w_out_temporal, v, 4), devices) for v in range(videos)]
        y = None
        for v in range(videos):
            y = cross_mlp(me, by_frame[v], modulation, k, v_t, w_query_cross, w_out_cross, w_mlp_in, w_mlp_out, v, y, videos)
        return y

    return jax.shard_map(local_block, mesh=mesh, in_specs=in_specs, out_specs=act_spec, check_vma=False)
```

time: 1230 us -> 830 us (0.67)
  Pallas kernels: 0 us -> 801 us
  matrix products: 744 us -> 0 us
  local copies, waits for them, and re-layouts: 185 us -> 2.56 us
  blocking collectives: 131 us -> 0 us
  waiting for transfers between devices: 112 us -> 0.06 us
  other arithmetic: 43.5 us -> 0 us
    pallas_call x0 -> x13, Pallas kernels: none -> 801 us  [the longest x4 381 us: cross_mlp(): pl.pallas_call(functools.partial(cross_mlp_kernel, heads=heads, dim=dim),...]
    dot_general x11 -> x0, matrix products: 581 us -> none  [the longest x1 95.8 us: cross_mlp(): jnp.einsum('btsc,cf->btsf', normed, w_mlp_in, preferred_element_type=jnp....]
    sub x2 -> x0, matrix products: 163 us -> none  [the longest x1 99.3 us: spatial_sublayer(): jax.nn.softmax(scores * head_dim ** (-0.5), axis=-1).astype(jnp.bfloat16)]
    all_to_all x1 -> x0, blocking collectives: 131 us -> none  [local_block(): by_patch = lax.all_to_all(after_spatial, 'sp', 2, 1, tiled=True)]
    all_to_all x1 -> x0, waiting for transfers between devices: 112 us -> none  [local_block(): by_frame = lax.all_to_all(after_temporal, 'sp', 1, 2, tiled=True)]
    squeeze x5 -> x0, local copies, waits for them, and re-layouts: 106 us -> none  [the longest x2 49.5 us: temporal_sublayer(): qkv_all[1]]
    convert_element_type x2 -> x0, local copies, waits for them, and re-layouts: 63.1 us -> none  [the longest x1 58.2 us: spatial_sublayer(): return (lat_f + mod_rows[2] * branch).astype(jnp.bfloat16)]
    reduce_sum x4 -> x0, other arithmetic: 41.9 us -> none  [the longest x1 21.1 us: cross_mlp(): jax.nn.softmax(scores * head_dim ** (-0.5), axis=-1).astype(jnp.bfloat16)]
  transfers between devices with their start and end apart: 1 -> 24, of which waited for: 1 -> 0; matrix products, arithmetic and copies ran while one was open for 1% -> 0% of each run, Pallas kernels for 0% -> 77%
where the time goes in v1:
time: 830 us; the launch traced here: 822 us
  Pallas kernels  801 us (97%)
  starting transfers between devices  18.3 us (2%)
    pallas_call x4, Pallas kernels, cross_mlp(): pl.pallas_call(functools.partial(cross_mlp_kernel, heads=heads, dim=dim),...  381 us
    pallas_call x4, Pallas kernels, spatial(): pl.pallas_call(functools.partial(spatial_kernel, heads=heads, dim=dim), g...  286 us
    pallas_call x4, Pallas kernels, temporal(): pl.pallas_call(functools.partial(temporal_kernel, heads=heads, dim=dim),...  120 us
    ppermute x24, starting transfers between devices, swap(): lax.ppermute(parts[d], 'sp', [(i, i ^ d) for i in range(devices)])  18.3 us
  transfers between devices with their start and end apart: 24, of which 0 were waited for; matrix products, arithmetic and copies ran while one was open for 0% of the time, Pallas kernels for 77%

profile of v1, /device:TPU:0, one launch (start us, length us, event | category | flops | bytes accessed | tf_op | source)
XLA Modules:
  0.0 822.2 jit_solution(4026051865839631660)
XLA Ops:
  0.0 1.6 copy.17.mod_ref
  1.6 71.4 %spatial.7 = (bf16[256,1408]{1,0:T(8,128)(2,1)}, bf16[256,1408]{1,0:T(8,128)(2,1)}, bf16[256,1408]{1,0:T(8,128)(2,1)}, bf16[256,1408]{1,0:T(8,128)(2,1)}) custom-call(s32[1]{0:T(128)} %bitcast.me_ref, bf16[4,1,1024,1408]{3,2,1,0:T(8,128)(2,1)} %x_ref.7, f32[4,6,1408]{2,1,0:T(8,128)} %copy.17.mod_ref, bf16[3,1408,1408]{2,1,0:T(8,128)(2,1)} %bitcast.9, ...), custom_call_target="tpu_custom_call" | custom-call | flops 22145925120 | bytes 21626880 | tf_op jit(solution)/shard_map/spatial/pallas_call | solution.py:260
  73.0 0.7 collective-permute-start.18
  73.7 2.5 collective-permute-start.19
  76.3 0.1 collective-permute-start.20
  76.3 71.5 %spatial.6 = (bf16[256,1408]{1,0:T(8,128)(2,1)}, bf16[256,1408]{1,0:T(8,128)(2,1)}, bf16[256,1408]{1,0:T(8,128)(2,1)}, bf16[256,1408]{1,0:T(8,128)(2,1)}) custom-call(s32[1]{0:T(128)} %bitcast.me_ref, bf16[4,1,1024,1408]{3,2,1,0:T(8,128)(2,1)} %x_ref.7, f32[4,6,1408]{2,1,0:T(8,128)} %copy.17.mod_ref, bf16[3,1408,1408]{2,1,0:T(8,128)(2,1)} %bitcast.10, ...), custom_call_target="tpu_custom_call" | custom-call | flops 22145925120 | bytes 21626880 | tf_op jit(solution)/shard_map/spatial/pallas_call | solution.py:260
  147.8 0.1 collective-permute-start.12
  148.0 1.9 collective-permute-start.13
  149.9 71.5 %spatial.5 = (bf16[256,1408]{1,0:T(8,128)(2,1)}, bf16[256,1408]{1,0:T(8,128)(2,1)}, bf16[256,1408]{1,0:T(8,128)(2,1)}, bf16[256,1408]{1,0:T(8,128)(2,1)}) custom-call(s32[1]{0:T(128)} %bitcast.me_ref, bf16[4,1,1024,1408]{3,2,1,0:T(8,128)(2,1)} %x_ref.7, f32[4,6,1408]{2,1,0:T(8,128)} %copy.17.mod_ref, bf16[3,1408,1408]{2,1,0:T(8,128)(2,1)} %bitcast.11, ...), custom_call_target="tpu_custom_call" | custom-call | flops 22145925120 | bytes 21626880 | tf_op jit(solution)/shard_map/spatial/pallas_call | solution.py:260
  221.5 71.8 %spatial.4 = (bf16[256,1408]{1,0:T(8,128)(2,1)}, bf16[256,1408]{1,0:T(8,128)(2,1)}, bf16[256,1408]{1,0:T(8,128)(2,1)}, bf16[256,1408]{1,0:T(8,128)(2,1)}) custom-call(s32[1]{0:T(128)} %bitcast.me_ref, bf16[4,1,1024,1408]{3,2,1,0:T(8,128)(2,1)} %x_ref.7, f32[4,6,1408]{2,1,0:T(8,128)} %copy.17.mod_ref, bf16[3,1408,1408]{2,1,0:T(8,128)(2,1)} %bitcast.12, ...), custom_call_target="tpu_custom_call" | custom-call | flops 22145925120 | bytes 21626880 | tf_op jit(solution)/shard_map/spatial/pallas_call | solution.py:260
  293.3 13.6 %text_kv.1 = (bf16[16,1024,88]{2,1,0:T(8,128)(2,1)}, bf16[16,88,1024]{2,1,0:T(8,128)(2,1)}) custom-call(bf16[1024,1408]{1,0:T(8,128)(2,1)} %bitcast.34, bf16[2,1408,1408]{2,1,0:T(8,128)(2,1)} %bitcast.17), custom_call_target="tpu_custom_call" | custom-call | flops 8120172544 | bytes 16580608 | tf_op jit(solution)/shard_map/text_kv/pallas_call | solution.py:313
  306.9 0.0 collective-permute-done.18.x1
  306.9 0.0 collective-permute-start.14
  307.0 0.0 collective-permute-done.19.x2
  307.0 0.2 collective-permute-start.6
  307.2 0.0 collective-permute-done.20.x3
  307.2 1.9 collective-permute-start.7
  309.1 0.0 copy-done.15
  309.1 29.9 %temporal.7 = (bf16[256,1408]{1,0:T(8,128)(2,1)}, bf16[256,1408]{1,0:T(8,128)(2,1)}, bf16[256,1408]{1,0:T(8,128)(2,1)}, bf16[256,1408]{1,0:T(8,128)(2,1)}) custom-call(s32[1]{0:T(128)} %bitcast.me_ref, bf16[256,1408]{1,0:T(8,128)(2,1)} %get-tuple-element.65.x0, bf16[256,1408]{1,0:T(8,128)(2,1)} %copy-done.14, bf16[256,1408]{1,0:T(8,128)(2,1)} %copy-done.15, ...), custom_call_target="tpu_custom_call" | custom-call | flops 16240345088 | bytes 21626880 | tf_op jit(solution)/shard_map/temporal/pallas_call | solution.py:297
  339.1 0.0 collective-permute-done.12.x1
  339.1 0.5 collective-permute-start.8
  339.6 0.0 collective-permute-done.13.x2
  339.6 0.0 collective-permute-start
  339.6 0.0 collective-permute-done.14.x3
  339.6 1.6 collective-permute-start.1
  341.3 30.1 %temporal.6 = (bf16[256,1408]{1,0:T(8,128)(2,1)}, bf16[256,1408]{1,0:T(8,128)(2,1)}, bf16[256,1408]{1,0:T(8,128)(2,1)}, bf16[256,1408]{1,0:T(8,128)(2,1)}) custom-call(s32[1]{0:T(128)} %bitcast.me_ref, bf16[256,1408]{1,0:T(8,128)(2,1)} %get-tuple-element.57.x0, bf16[256,1408]{1,0:T(8,128)(2,1)} %copy-done.12, bf16[256,1408]{1,0:T(8,128)(2,1)} %copy-done.13, ...), custom_call_target="tpu_custom_call" | custom-call | flops 16240345088 | bytes 21626880 | tf_op jit(solution)/shard_map/temporal/pallas_call | solution.py:297
  371.4 0.0 collective-permute-done.6.x1
  371.4 0.5 collective-permute-start.2
  371.9 0.0 collective-permute-done.7.x2
  371.9 0.1 collective-permute-start.21
  372.0 0.0 collective-permute-done.8.x3
  372.0 1.6 collective-permute-start.22
  373.6 30.1 %temporal.5 = (bf16[256,1408]{1,0:T(8,128)(2,1)}, bf16[256,1408]{1,0:T(8,128)(2,1)}, bf16[256,1408]{1,0:T(8,128)(2,1)}, bf16[256,1408]{1,0:T(8,128)(2,1)}) custom-call(s32[1]{0:T(128)} %bitcast.me_ref, bf16[256,1408]{1,0:T(8,128)(2,1)} %get-tuple-element.49.x0, bf16[256,1408]{1,0:T(8,128)(2,1)} %collective-permute-done.6.x1, ...), custom_call_target="tpu_custom_call" | custom-call | flops 16240345088 | bytes 21626880 | tf_op jit(solution)/shard_map/temporal/pallas_call | solution.py:297
  403.8 0.0 collective-permute-done.x1
  403.8 0.2 collective-permute-start.23
  404.0 0.0 collective-permute-done.1.x2
  404.0 0.3 collective-permute-start.15
  404.3 0.0 collective-permute-done.2.x3
  404.3 1.6 collective-permute-start.16
  406.0 30.2 %temporal.4 = (bf16[256,1408]{1,0:T(8,128)(2,1)}, bf16[256,1408]{1,0:T(8,128)(2,1)}, bf16[256,1408]{1,0:T(8,128)(2,1)}, bf16[256,1408]{1,0:T(8,128)(2,1)}) custom-call(s32[1]{0:T(128)} %bitcast.me_ref, bf16[256,1408]{1,0:T(8,128)(2,1)} %get-tuple-element.39.x0, bf16[256,1408]{1,0:T(8,128)(2,1)} %collective-permute-done.x1, ...), custom_call_target="tpu_custom_call" | custom-call | flops 16240345088 | bytes 21626880 | tf_op jit(solution)/shard_map/temporal/pallas_call | solution.py:297
  436.2 0.0 collective-permute-done.21.x1
  436.2 0.0 collective-permute-start.17
  436.2 0.0 collective-permute-done.22.x2
  436.2 1.4 collective-permute-start.10
  437.6 0.0 collective-permute-done.23.x3
  437.6 0.5 collective-permute-start.11
  438.1 95.2 %cross_mlp.4.rest_0_ = bf16[4,1,1024,1408]{3,2,1,0:T(8,128)(2,1)} custom-call(s32[1]{0:T(128)} %bitcast.me_ref, bf16[256,1408]{1,0:T(8,128)(2,1)} %get-tuple-element.69.x0, bf16[256,1408]{1,0:T(8,128)(2,1)} %collective-permute-done.21.x1, bf16[256,1408]{1,0:T(8,128)(2,1)} %collective-permute-done.22.x2, bf16[256,1408]{1,0:T(8,128)(2,1)} %collective-permute-done.23.x3, ...), custom_call_target="tpu_custom_call" | custom-call | flops 42077257728 | bytes 45416448 | tf_op jit(solution)/shard_map/cross_mlp/pallas_call | solution.py:365
  533.3 0.0 collective-permute-done.15.x1
  533.3 0.4 collective-permute-start.9
  533.7 0.0 collective-permute-done.16.x2
  533.7 0.2 collective-permute-start.3
  533.9 0.0 collective-permute-done.17.x3
  533.9 1.6 collective-permute-start.4
  535.5 95.3 %cross_mlp.5.rest_0_ = bf16[4,1,1024,1408]{3,2,1,0:T(8,128)(2,1)} custom-call(s32[1]{0:T(128)} %bitcast.me_ref, bf16[256,1408]{1,0:T(8,128)(2,1)} %get-tuple-element.61.x0, bf16[256,1408]{1,0:T(8,128)(2,1)} %collective-permute-done.15.x1, bf16[256,1408]{1,0:T(8,128)(2,1)} %collective-permute-done.16.x2, ...), custom_call_target="tpu_custom_call", output_to_operand_aliasing={{}: (12, {})} | custom-call | flops 42077257728 | bytes 45416448 | tf_op jit(solution)/shard_map/cross_mlp/pallas_call | solution.py:365
  630.7 0.0 collective-permute-done.10.x2
  630.8 0.1 collective-permute-start.5
  630.9 0.0 collective-permute-done.11.x3
  630.9 0.0 collective-permute-done.9.x1
  630.9 95.0 %cross_mlp.6.rest_0_ = bf16[4,1,1024,1408]{3,2,1,0:T(8,128)(2,1)} custom-call(s32[1]{0:T(128)} %bitcast.me_ref, bf16[256,1408]{1,0:T(8,128)(2,1)} %get-tuple-element.53.x0, bf16[256,1408]{1,0:T(8,128)(2,1)} %collective-permute-done.9.x1, bf16[256,1408]{1,0:T(8,128)(2,1)} %collective-permute-done.10.x2, ...), custom_call_target="tpu_custom_call", output_to_operand_aliasing={{}: (12, {})} | custom-call | flops 42077257728 | bytes 45416448 | tf_op jit(solution)/shard_map/cross_mlp/pallas_call | solution.py:365
  725.9 0.0 collective-permute-done.3.x1
  725.9 0.0 collective-permute-done.4.x2
  725.9 0.0 collective-permute-done.5.x3
  725.9 0.9 copy-done.16
  726.9 95.1 %cross_mlp.7 = bf16[4,1,1024,1408]{3,2,1,0:T(8,128)(2,1)} custom-call(s32[1]{0:T(128)} %bitcast.me_ref, bf16[256,1408]{1,0:T(8,128)(2,1)} %get-tuple-element.43.x0, bf16[256,1408]{1,0:T(8,128)(2,1)} %collective-permute-done.3.x1, bf16[256,1408]{1,0:T(8,128)(2,1)} %copy-done.16, ...), custom_call_target="tpu_custom_call", output_to_operand_aliasing={{}: (12, {})} | custom-call | flops 42077257728 | bytes 45416448 | tf_op jit(solution)/shard_map/cross_mlp/pallas_call | solution.py:365
  (32 shorter events, 0.1 us)
Async XLA Ops:
  73.0 233.9 %collective-permute-start.18 = (bf16[256,1408]{1,0:T(8,128)(2,1)}, bf16[256,1408]{1,0:T(8,128)(2,1)S(1)}, u32[]{:S(2)}, u32[]{:S(2)}) collective-permute-start(bf16[256,1408]{1,0:T(8,128)(2,1)} %get-tuple-element.66), channel_id=1, source_target_pairs={{0,1},{1,0},{2,3},{3,2},{4,5},{5,4},{6,7},{7,6},{8,9},{9,8},{10,11... | collective-permute-start | bytes 2162696 | tf_op jit(solution)/shard_map/ppermute | solution.py:377
  73.7 233.2 %collective-permute-start.19 = (bf16[256,1408]{1,0:T(8,128)(2,1)}, bf16[256,1408]{1,0:T(8,128)(2,1)S(1)}, u32[]{:S(2)}, u32[]{:S(2)}) collective-permute-start(bf16[256,1408]{1,0:T(8,128)(2,1)} %get-tuple-element.67), channel_id=1, source_target_pairs={{0,2},{1,3},{2,0},{3,1},{4,6},{5,7},{6,4},{7,5},{8,10},{9,11},{10,... | collective-permute-start | bytes 2162696 | tf_op jit(solution)/shard_map/ppermute | solution.py:377
  76.3 230.9 %collective-permute-start.20 = (bf16[256,1408]{1,0:T(8,128)(2,1)}, bf16[256,1408]{1,0:T(8,128)(2,1)}, u32[]{:S(2)}, u32[]{:S(2)}) collective-permute-start(bf16[256,1408]{1,0:T(8,128)(2,1)} %get-tuple-element.68), channel_id=1, source_target_pairs={{0,3},{1,2},{2,1},{3,0},{4,7},{5,6},{6,5},{7,4},{8,11},{9,10},{10,... | collective-permute-start | bytes 2162696 | tf_op jit(solution)/shard_map/ppermute | solution.py:377
  147.8 191.2 %collective-permute-start.12 = (bf16[256,1408]{1,0:T(8,128)(2,1)}, bf16[256,1408]{1,0:T(8,128)(2,1)S(1)}, u32[]{:S(2)}, u32[]{:S(2)}) collective-permute-start(bf16[256,1408]{1,0:T(8,128)(2,1)} %get-tuple-element.58), channel_id=1, source_target_pairs={{0,1},{1,0},{2,3},{3,2},{4,5},{5,4},{6,7},{7,6},{8,9},{9,8},{10,11... | collective-permute-start | bytes 2162696 | tf_op jit(solution)/shard_map/ppermute | solution.py:377
  148.0 191.6 %collective-permute-start.13 = (bf16[256,1408]{1,0:T(8,128)(2,1)}, bf16[256,1408]{1,0:T(8,128)(2,1)S(1)}, u32[]{:S(2)}, u32[]{:S(2)}) collective-permute-start(bf16[256,1408]{1,0:T(8,128)(2,1)} %get-tuple-element.59), channel_id=1, source_target_pairs={{0,2},{1,3},{2,0},{3,1},{4,6},{5,7},{6,4},{7,5},{8,10},{9,11},{10,... | collective-permute-start | bytes 2162696 | tf_op jit(solution)/shard_map/ppermute | solution.py:377
  293.3 13.9 %copy-start.11 = (bf16[256,1408]{1,0:T(8,128)(2,1)S(1)}, bf16[256,1408]{1,0:T(8,128)(2,1)}, u32[]{:S(2)}) copy-start(bf16[256,1408]{1,0:T(8,128)(2,1)} %get-tuple-element.51) | copy-start | bytes 2162692
  306.9 2.2 copy-start.14
  306.9 32.7 %collective-permute-start.14 = (bf16[256,1408]{1,0:T(8,128)(2,1)}, bf16[256,1408]{1,0:T(8,128)(2,1)}, u32[]{:S(2)}, u32[]{:S(2)}) collective-permute-start(bf16[256,1408]{1,0:T(8,128)(2,1)} %get-tuple-element.60), channel_id=1, source_target_pairs={{0,3},{1,2},{2,1},{3,0},{4,7},{5,6},{6,5},{7,4},{8,11},{9,10},{10,... | collective-permute-start | bytes 2162696 | tf_op jit(solution)/shard_map/ppermute | solution.py:377
  307.0 2.1 copy-start.15
  307.0 64.4 %collective-permute-start.6 = (bf16[256,1408]{1,0:T(8,128)(2,1)}, bf16[256,1408]{1,0:T(8,128)(2,1)}, u32[]{:S(2)}, u32[]{:S(2)}) collective-permute-start(bf16[256,1408]{1,0:T(8,128)(2,1)} %get-tuple-element.50), channel_id=1, source_target_pairs={{0,1},{1,0},{2,3},{3,2},{4,5},{5,4},{6,7},{7,6},{8,9},{9,8},{10,11... | collective-permute-start | bytes 2162696 | tf_op jit(solution)/shard_map/ppermute | solution.py:377
  307.2 64.8 %collective-permute-start.7 = (bf16[256,1408]{1,0:T(8,128)(2,1)S(1)}, bf16[256,1408]{1,0:T(8,128)(2,1)}, u32[]{:S(2)}, u32[]{:S(2)}) collective-permute-start(bf16[256,1408]{1,0:T(8,128)(2,1)S(1)} %copy-done.11), channel_id=1, source_target_pairs={{0,2},{1,3},{2,0},{3,1},{4,6},{5,7},{6,4},{7,5},{8,10},{9,11},{10,... | collective-permute-start | bytes 2162696 | tf_op jit(solution)/shard_map/ppermute | solution.py:377
  309.1 30.0 %copy-start.10 = (bf16[256,1408]{1,0:T(8,128)(2,1)S(1)}, bf16[256,1408]{1,0:T(8,128)(2,1)}, u32[]{:S(2)}) copy-start(bf16[256,1408]{1,0:T(8,128)(2,1)} %get-tuple-element.52) | copy-start | bytes 2162692
  309.1 30.5 %copy-start.4 = (bf16[256,1408]{1,0:T(8,128)(2,1)S(1)}, bf16[256,1408]{1,0:T(8,128)(2,1)}, u32[]{:S(2)}) copy-start(bf16[256,1408]{1,0:T(8,128)(2,1)} %get-tuple-element.41) | copy-start | bytes 2162692
  339.1 2.2 copy-start.12
  339.1 32.9 %collective-permute-start.8 = (bf16[256,1408]{1,0:T(8,128)(2,1)S(1)}, bf16[256,1408]{1,0:T(8,128)(2,1)}, u32[]{:S(2)}, u32[]{:S(2)}) collective-permute-start(bf16[256,1408]{1,0:T(8,128)(2,1)S(1)} %copy-done.10), channel_id=1, source_target_pairs={{0,3},{1,2},{2,1},{3,0},{4,7},{5,6},{6,5},{7,4},{8,11},{9,10},{10,... | collective-permute-start | bytes 2162696 | tf_op jit(solution)/shard_map/ppermute | solution.py:377
  339.6 1.7 copy-start.13
  339.6 64.1 %collective-permute-start = (bf16[256,1408]{1,0:T(8,128)(2,1)}, bf16[256,1408]{1,0:T(8,128)(2,1)}, u32[]{:S(2)}, u32[]{:S(2)}) collective-permute-start(bf16[256,1408]{1,0:T(8,128)(2,1)} %get-tuple-element.40), channel_id=1, source_target_pairs={{0,1},{1,0},{2,3},{3,2},{4,5},{5,4},{6,7},{7,6},{8,9},{9,8},{10,11... | collective-permute-start | bytes 2162696 | tf_op jit(solution)/shard_map/ppermute | solution.py:377
  339.6 64.4 %collective-permute-start.1 = (bf16[256,1408]{1,0:T(8,128)(2,1)S(1)}, bf16[256,1408]{1,0:T(8,128)(2,1)}, u32[]{:S(2)}, u32[]{:S(2)}) collective-permute-start(bf16[256,1408]{1,0:T(8,128)(2,1)S(1)} %copy-done.4), channel_id=1, source_target_pairs={{0,2},{1,3},{2,0},{3,1},{4,6},{5,7},{6,4},{7,5},{8,10},{9,11},{10,... | collective-permute-start | bytes 2162696 | tf_op jit(solution)/shard_map/ppermute | solution.py:377
  341.3 30.1 %copy-start.1 = (bf16[256,1408]{1,0:T(8,128)(2,1)S(1)}, bf16[256,1408]{1,0:T(8,128)(2,1)}, u32[]{:S(2)}) copy-start(bf16[256,1408]{1,0:T(8,128)(2,1)} %get-tuple-element.42) | copy-start | bytes 2162692
  341.3 30.7 %copy-start.3 = (bf16[256,1408]{1,0:T(8,128)(2,1)S(1)}, bf16[256,1408]{1,0:T(8,128)(2,1)}, u32[]{:S(2)}) copy-start(bf16[256,1408]{1,0:T(8,128)(2,1)} %get-tuple-element.71) | copy-start | bytes 2162692
  371.4 32.9 %collective-permute-start.2 = (bf16[256,1408]{1,0:T(8,128)(2,1)S(1)}, bf16[256,1408]{1,0:T(8,128)(2,1)}, u32[]{:S(2)}, u32[]{:S(2)}) collective-permute-start(bf16[256,1408]{1,0:T(8,128)(2,1)S(1)} %copy-done.1), channel_id=1, source_target_pairs={{0,3},{1,2},{2,1},{3,0},{4,7},{5,6},{6,5},{7,4},{8,11},{9,10},{10,... | collective-permute-start | bytes 2162696 | tf_op jit(solution)/shard_map/ppermute | solution.py:377
  371.9 64.2 %collective-permute-start.21 = (bf16[256,1408]{1,0:T(8,128)(2,1)}, bf16[256,1408]{1,0:T(8,128)(2,1)}, u32[]{:S(2)}, u32[]{:S(2)}) collective-permute-start(bf16[256,1408]{1,0:T(8,128)(2,1)} %get-tuple-element.70), channel_id=1, source_target_pairs={{0,1},{1,0},{2,3},{3,2},{4,5},{5,4},{6,7},{7,6},{8,9},{9,8},{10,11... | collective-permute-start | bytes 2162696 | tf_op jit(solution)/shard_map/ppermute | solution.py:377
  372.0 64.2 %collective-permute-start.22 = (bf16[256,1408]{1,0:T(8,128)(2,1)S(1)}, bf16[256,1408]{1,0:T(8,128)(2,1)}, u32[]{:S(2)}, u32[]{:S(2)}) collective-permute-start(bf16[256,1408]{1,0:T(8,128)(2,1)S(1)} %copy-done.3), channel_id=1, source_target_pairs={{0,2},{1,3},{2,0},{3,1},{4,6},{5,7},{6,4},{7,5},{8,10},{9,11},{10,... | collective-permute-start | bytes 2162696 | tf_op jit(solution)/shard_map/ppermute | solution.py:377
  373.6 30.2 %copy-start = (bf16[256,1408]{1,0:T(8,128)(2,1)S(1)}, bf16[256,1408]{1,0:T(8,128)(2,1)}, u32[]{:S(2)}) copy-start(bf16[256,1408]{1,0:T(8,128)(2,1)} %get-tuple-element.72) | copy-start | bytes 2162692
  373.6 30.7 %copy-start.5 = (bf16[256,1408]{1,0:T(8,128)(2,1)S(1)}, bf16[256,1408]{1,0:T(8,128)(2,1)}, u32[]{:S(2)}) copy-start(bf16[256,1408]{1,0:T(8,128)(2,1)} %get-tuple-element.63) | copy-start | bytes 2162692
  403.8 33.8 %collective-permute-start.23 = (bf16[256,1408]{1,0:T(8,128)(2,1)S(1)}, bf16[256,1408]{1,0:T(8,128)(2,1)}, u32[]{:S(2)}, u32[]{:S(2)}) collective-permute-start(bf16[256,1408]{1,0:T(8,128)(2,1)S(1)} %copy-done), channel_id=1, source_target_pairs={{0,3},{1,2},{2,1},{3,0},{4,7},{5,6},{6,5},{7,4},{8,11},{9,10},{10,... | collective-permute-start | bytes 2162696 | tf_op jit(solution)/shard_map/ppermute | solution.py:377
  404.0 129.3 %collective-permute-start.15 = (bf16[256,1408]{1,0:T(8,128)(2,1)}, bf16[256,1408]{1,0:T(8,128)(2,1)}, u32[]{:S(2)}, u32[]{:S(2)}) collective-permute-start(bf16[256,1408]{1,0:T(8,128)(2,1)} %get-tuple-element.62), channel_id=1, source_target_pairs={{0,1},{1,0},{2,3},{3,2},{4,5},{5,4},{6,7},{7,6},{8,9},{9,8},{10,11... | collective-permute-start | bytes 2162696 | tf_op jit(solution)/shard_map/ppermute | solution.py:377
  404.3 129.3 %collective-permute-start.16 = (bf16[256,1408]{1,0:T(8,128)(2,1)S(1)}, bf16[256,1408]{1,0:T(8,128)(2,1)}, u32[]{:S(2)}, u32[]{:S(2)}) collective-permute-start(bf16[256,1408]{1,0:T(8,128)(2,1)S(1)} %copy-done.5), channel_id=1, source_target_pairs={{0,2},{1,3},{2,0},{3,1},{4,6},{5,7},{6,4},{7,5},{8,10},{9,11},{10,... | collective-permute-start | bytes 2162696 | tf_op jit(solution)/shard_map/ppermute | solution.py:377
  406.0 30.2 %copy-start.2 = (bf16[256,1408]{1,0:T(8,128)(2,1)S(1)}, bf16[256,1408]{1,0:T(8,128)(2,1)}, u32[]{:S(2)}) copy-start(bf16[256,1408]{1,0:T(8,128)(2,1)} %get-tuple-element.64) | copy-start | bytes 2162692
  406.0 31.7 %copy-start.7 = (bf16[256,1408]{1,0:T(8,128)(2,1)S(1)}, bf16[256,1408]{1,0:T(8,128)(2,1)}, u32[]{:S(2)}) copy-start(bf16[256,1408]{1,0:T(8,128)(2,1)} %get-tuple-element.56) | copy-start | bytes 2162692
  436.2 97.7 %collective-permute-start.17 = (bf16[256,1408]{1,0:T(8,128)(2,1)S(1)}, bf16[256,1408]{1,0:T(8,128)(2,1)}, u32[]{:S(2)}, u32[]{:S(2)}) collective-permute-start(bf16[256,1408]{1,0:T(8,128)(2,1)S(1)} %copy-done.2), channel_id=1, source_target_pairs={{0,3},{1,2},{2,1},{3,0},{4,7},{5,6},{6,5},{7,4},{8,11},{9,10},{10,... | collective-permute-start | bytes 2162696 | tf_op jit(solution)/shard_map/ppermute | solution.py:377
  436.2 194.5 %collective-permute-start.10 = (bf16[256,1408]{1,0:T(8,128)(2,1)}, bf16[256,1408]{1,0:T(8,128)(2,1)}, u32[]{:S(2)}, u32[]{:S(2)}) collective-permute-start(bf16[256,1408]{1,0:T(8,128)(2,1)} %get-tuple-element.55), channel_id=1, source_target_pairs={{0,2},{1,3},{2,0},{3,1},{4,6},{5,7},{6,4},{7,5},{8,10},{9,11},{10,... | collective-permute-start | bytes 2162696 | tf_op jit(solution)/shard_map/ppermute | solution.py:377
  437.6 193.2 %collective-permute-start.11 = (bf16[256,1408]{1,0:T(8,128)(2,1)S(1)}, bf16[256,1408]{1,0:T(8,128)(2,1)}, u32[]{:S(2)}, u32[]{:S(2)}) collective-permute-start(bf16[256,1408]{1,0:T(8,128)(2,1)S(1)} %copy-done.7), channel_id=1, source_target_pairs={{0,3},{1,2},{2,1},{3,0},{4,7},{5,6},{6,5},{7,4},{8,11},{9,10},{10,... | collective-permute-start | bytes 2162696 | tf_op jit(solution)/shard_map/ppermute | solution.py:377
  438.1 95.2 %copy-start.6 = (bf16[256,1408]{1,0:T(8,128)(2,1)S(1)}, bf16[256,1408]{1,0:T(8,128)(2,1)}, u32[]{:S(2)}) copy-start(bf16[256,1408]{1,0:T(8,128)(2,1)} %get-tuple-element.54) | copy-start | bytes 2162692
  438.1 95.8 %copy-start.9 = (bf16[256,1408]{1,0:T(8,128)(2,1)S(1)}, bf16[256,1408]{1,0:T(8,128)(2,1)}, u32[]{:S(2)}) copy-start(bf16[256,1408]{1,0:T(8,128)(2,1)} %get-tuple-element.45) | copy-start | bytes 2162692
  533.3 97.6 %collective-permute-start.9 = (bf16[256,1408]{1,0:T(8,128)(2,1)S(1)}, bf16[256,1408]{1,0:T(8,128)(2,1)}, u32[]{:S(2)}, u32[]{:S(2)}) collective-permute-start(bf16[256,1408]{1,0:T(8,128)(2,1)S(1)} %copy-done.6), channel_id=1, source_target_pairs={{0,1},{1,0},{2,3},{3,2},{4,5},{5,4},{6,7},{7,6},{8,9},{9,8},{10,11... | collective-permute-start | bytes 2162696 | tf_op jit(solution)/shard_map/ppermute | solution.py:377
  533.7 192.2 %collective-permute-start.3 = (bf16[256,1408]{1,0:T(8,128)(2,1)}, bf16[256,1408]{1,0:T(8,128)(2,1)}, u32[]{:S(2)}, u32[]{:S(2)}) collective-permute-start(bf16[256,1408]{1,0:T(8,128)(2,1)} %get-tuple-element.44), channel_id=1, source_target_pairs={{0,1},{1,0},{2,3},{3,2},{4,5},{5,4},{6,7},{7,6},{8,9},{9,8},{10,11... | collective-permute-start | bytes 2162696 | tf_op jit(solution)/shard_map/ppermute | solution.py:377
  533.9 192.1 %collective-permute-start.4 = (bf16[256,1408]{1,0:T(8,128)(2,1)S(1)}, bf16[256,1408]{1,0:T(8,128)(2,1)S(1)}, u32[]{:S(2)}, u32[]{:S(2)}) collective-permute-start(bf16[256,1408]{1,0:T(8,128)(2,1)S(1)} %copy-done.9), channel_id=1, source_target_pairs={{0,2},{1,3},{2,0},{3,1},{4,6},{5,7},{6,4},{7,5},{8,10},{9,11},{10,... | collective-permute-start | bytes 2162696 | tf_op jit(solution)/shard_map/ppermute | solution.py:377
  535.5 95.3 %copy-start.8 = (bf16[256,1408]{1,0:T(8,128)(2,1)S(1)}, bf16[256,1408]{1,0:T(8,128)(2,1)}, u32[]{:S(2)}) copy-start(bf16[256,1408]{1,0:T(8,128)(2,1)} %get-tuple-element.46) | copy-start | bytes 2162692
  630.8 95.2 %collective-permute-start.5 = (bf16[256,1408]{1,0:T(8,128)(2,1)S(1)}, bf16[256,1408]{1,0:T(8,128)(2,1)}, u32[]{:S(2)}, u32[]{:S(2)}) collective-permute-start(bf16[256,1408]{1,0:T(8,128)(2,1)S(1)} %copy-done.8), channel_id=1, source_target_pairs={{0,3},{1,2},{2,1},{3,0},{4,7},{5,6},{6,5},{7,4},{8,11},{9,10},{10,... | collective-permute-start | bytes 2162696 | tf_op jit(solution)/shard_map/ppermute | solution.py:377
  725.9 0.9 copy-start.16

commit v2 on v1

--- a/solution.py
+++ b/solution.py
@@ -50,14 +50,46 @@
     lax.fori_loop(0, tokens // chunk, body, 0)
 
 
-def attend_block(k, v_t, q_t, scale):
-    s = dot(k, q_t)
-    p = jnp.exp2((s - jnp.max(s, axis=0, keepdims=True)) * scale)
-    total = jnp.sum(p, axis=0, keepdims=True)
-    return dot(v_t, p.astype(BF16)) / total
-
-
-def spatial_kernel(me_ref, x_ref, mod_ref, w_ref, wo_hbm, o0, o1, o2, o3, u_s, q_s, k_s, v_s, a_s, wo_s, sem, *, heads, dim):
+def attend_heads(q, k, v, out, scores, probs, base, row, scale, count, block):
+    tokens, keys, dim = out.shape[1], k.shape[1], v.shape[1]
+    chunk = min(256, keys)
+    blocks = [(h, c) for c in range(tokens // block) for h in range(count)]
+    tops, mixed = {}, {}
+
+    def score(n):
+        h, c = blocks[n]
+        top = None
+        for r in range(0, keys, chunk):
+            s = dot(k[base + h, r:r + chunk, :], q[base + h, :, c * block:(c + 1) * block])
+            scores[n % 2][r:r + chunk, :] = s
+            part = jnp.max(s.reshape(chunk // 8, 8, block), axis=0)
+            top = part if top is None else jnp.maximum(top, part)
+        tops[n] = jnp.max(top, axis=0, keepdims=True)
+
+    def mix(n):
+        h, c = blocks[n]
+        total = None
+        for r in range(0, keys, chunk):
+            p = jnp.exp2((scores[n % 2][r:r + chunk, :] - tops[n]) * scale)
+            part = jnp.sum(p.reshape(chunk // 8, 8, block), axis=0)
+            total = part if total is None else total + part
+            probs[n % 2][r:r + chunk, :] = p.astype(BF16)
+        mixed[h] = dot(v[base + h], probs[n % 2][...]) / jnp.sum(total, axis=0, keepdims=True)
+        if h == count - 1:
+            out[pl.ds(row, count * dim), c * block:(c + 1) * block] = jnp.concatenate([mixed[i] for i in range(count)], axis=0).astype(BF16)
+
+    score(0)
+    for n in range(len(blocks)):
+        if n + 1 < len(blocks):
+            score(n + 1)
+        mix(n)
+
+
+def gelu(x):
+    return x * (0.5 + 0.5 * jnp.tanh(x * (0.7978845608028654 + 0.7978845608028654 * 0.044715 * (x * x))))
+
+
+def spatial_kernel(me_ref, x_ref, mod_ref, w_ref, wo_hbm, o0, o1, o2, o3, u_s, q_s, k_s, v_s, a_s, wo_s, s0, s1, p0, p1, sem, *, heads, dim):
     g = pl.program_id(0)
     tokens = x_ref.shape[0]
     quarter = tokens // 4
@@ -66,7 +98,6 @@
 
     @pl.when(g == 0)
     def _():
-        wo_copy.start()
         q_s[:, dim:, :] = jnp.zeros((heads, q_s.shape[1] - dim, tokens), BF16)
         k_s[:, :, dim:] = jnp.zeros((heads, tokens, k_s.shape[2] - dim), BF16)
 
@@ -79,12 +110,13 @@
 
     project_heads(w_ref, u_s, q_s, k_s, v_s, heads, dim, 512)
 
+    @pl.when(g == 1)
+    def _():
+        wo_copy.start()
+
     def pair(i, carry):
-        rows = pl.ds(pl.multiple_of((g * heads + 2 * i) * dim, 2 * dim), 2 * dim)
-        for c in range(4):
-            cols = slice(c * quarter, (c + 1) * quarter)
-            outs = [attend_block(k_s[2 * i + h], v_s[2 * i + h], q_s[2 * i + h, :, cols], scale) for h in range(2)]
-            a_s[rows, cols] = jnp.concatenate(outs, axis=0).astype(BF16)
+        row = pl.multiple_of((g * heads + 2 * i) * dim, 2 * dim)
+        attend_heads(q_s, k_s, v_s, a_s, (s0, s1), (p0, p1), 2 * i, row, scale, 2, 512)
         return carry
 
     lax.fori_loop(0, heads // 2, pair, 0)
@@ -107,7 +139,6 @@
 
     @pl.when(g == 0)
     def _():
-        wo_copy.start()
         for d, x in enumerate(frames):
             pos = pos_ref[pl.ds(jnp.bitwise_xor(me_ref[0], d), 1), :]
             z_s[d * quarter:(d + 1) * quarter, :] = (x[...].astype(F32) + pos).astype(BF16)
@@ -120,6 +151,10 @@
         return carry
 
     lax.fori_loop(0, z_s.shape[0] // 512, proj, 0)
+
+    @pl.when(g == 1)
+    def _():
+        wo_copy.start()
 
     def attend(h, cols):
         outs = []
@@ -159,12 +194,13 @@
     tokens = t_ref.shape[0]
     k_t = dot(w_ref[0], t_ref[...], NT)
     v_ref[...] = dot(w_ref[1], t_ref[...], NT).reshape(heads, dim, tokens).astype(BF16)
+    k_ref[:, :, dim:] = jnp.zeros((heads, tokens, k_ref.shape[2] - dim), BF16)
     for h in range(heads):
-        k_ref[h] = k_t[h * dim:(h + 1) * dim].T.astype(BF16)
+        k_ref[h, :, :dim] = k_t[h * dim:(h + 1) * dim].T.astype(BF16)
 
 
 def cross_mlp_kernel(me_ref, x0, x1, x2, x3, mod_ref, k_ref, v_ref, wq_hbm, wo_hbm, w_in, w_out, *rest, heads, dim):
-    y_ref, q_s, a_s, h_s, u_s, acc_s, wq_s, wo_s, sems = rest[-9:]
+    y_ref, q_s, a_s, h_s, u_s, acc_s, wq_s, wo_s, s0, s1, p0, p1, sems = rest[-13:]
     step = pl.program_id(0)
     quarter = x0.shape[0]
     tokens = 4 * quarter
@@ -172,6 +208,7 @@
 
     @pl.when(step == 0)
     def _():
+        acc_s[...] = jnp.zeros_like(acc_s)
         q_copy = pltpu.make_async_copy(wq_hbm, wq_s, sems.at[0])
         o_copy = pltpu.make_async_copy(wo_hbm, wo_s, sems.at[1])
         q_copy.start()
@@ -179,17 +216,15 @@
         q_copy.wait()
         for d, x in enumerate((x0, x1, x2, x3)):
             cols = slice(d * quarter, (d + 1) * quarter)
-            q_s[:, :, cols] = dot(wq_s[...], x[...], NT).reshape(heads, dim, quarter).astype(BF16)
-
-        def pair(i, carry):
-            rows = pl.ds(pl.multiple_of(2 * i * dim, 2 * dim), 2 * dim)
-            for d in range(4):
-                cols = slice(d * quarter, (d + 1) * quarter)
-                outs = [attend_block(k_ref[2 * i + h], v_ref[2 * i + h], q_s[2 * i + h, :, cols], scale) for h in range(2)]
-                a_s[rows, cols] = jnp.concatenate(outs, axis=0).astype(BF16)
+            q_s[:, :dim, cols] = dot(wq_s[...], x[...], NT).reshape(heads, dim, quarter).astype(BF16)
+        q_s[:, dim:, :] = jnp.zeros((heads, q_s.shape[1] - dim, tokens), BF16)
+
+        def four(i, carry):
+            row = pl.multiple_of(4 * i * dim, 4 * dim)
+            attend_heads(q_s, k_ref, v_ref, a_s, (s0, s1), (p0, p1), 4 * i, row, scale, 4, 512)
             return carry
 
-        lax.fori_loop(0, heads // 2, pair, 0)
+        lax.fori_loop(0, heads // 4, four, 0)
         o_copy.wait()
         for d, x in enumerate((x0, x1, x2, x3)):
             rows = slice(d * quarter, (d + 1) * quarter)
@@ -198,22 +233,8 @@
             h_s[rows, :] = after
             u_s[rows, :] = normed_rows(after, mod_ref[3:4, :], mod_ref[4:5, :])
 
-    def mlp(i, carry):
-        rows = pl.ds(pl.multiple_of(i * 256, 256), 256)
-        hidden = jax.nn.gelu(dot(u_s[rows, :], w_in[...]), approximate=True).astype(BF16)
-        part = dot(hidden, w_out[...])
-
-        @pl.when(step == 0)
-        def _():
-            acc_s[rows, :] = part
-
-        @pl.when(step > 0)
-        def _():
-            acc_s[rows, :] += part
-
-        return carry
-
-    lax.fori_loop(0, tokens // 256, mlp, 0)
+    hidden = gelu(dot(u_s[...], w_in[...])).astype(BF16)
+    acc_s[...] += dot(hidden, w_out[...])
 
     @pl.when(step == pl.num_programs(0) - 1)
     def _():
@@ -254,6 +275,10 @@
             pltpu.VMEM((heads, dim, tokens), BF16),
             pltpu.VMEM((total, tokens), BF16),
             pltpu.VMEM((total, width), BF16),
+            pltpu.VMEM((tokens, 512), F32),
+            pltpu.VMEM((tokens, 512), F32),
+            pltpu.VMEM((tokens, 512), BF16),
+            pltpu.VMEM((tokens, 512), BF16),
             pltpu.SemaphoreType.DMA,
         ],
     )
@@ -314,8 +339,8 @@
         functools.partial(text_kernel, heads=heads, dim=dim),
         grid=(count // heads,),
         in_specs=[resident((tokens, width)), pl.BlockSpec((2, heads * dim, width), lambda g: (0, g, 0))],
-        out_specs=[pl.BlockSpec((heads, tokens, dim), lambda g: (g, 0, 0)), pl.BlockSpec((heads, dim, tokens), lambda g: (g, 0, 0))],
-        out_shape=[jax.ShapeDtypeStruct((count, tokens, dim), BF16), jax.ShapeDtypeStruct((count, dim, tokens), BF16)],
+        out_specs=[pl.BlockSpec((heads, tokens, 128), lambda g: (g, 0, 0)), pl.BlockSpec((heads, dim, tokens), lambda g: (g, 0, 0))],
+        out_shape=[jax.ShapeDtypeStruct((count, tokens, 128), BF16), jax.ShapeDtypeStruct((count, dim, tokens), BF16)],
         compiler_params=params(),
         cost_estimate=cost(4 * tokens * width * total, 2 * (2 * total * width + 3 * tokens * width)),
         name="text_kv",
@@ -325,7 +350,7 @@
 def cross_mlp(me, chunks, modulation, k, v_t, w_query, w_out_cross, w_in, w_out, v, y, videos):
     quarter, width = chunks[0].shape
     tokens = 4 * quarter
-    heads, all_text, dim = k.shape
+    heads, dim, all_text = v_t.shape
     text = all_text // videos
     total = heads * dim
     hidden = w_in.shape[1]
@@ -333,7 +358,7 @@
     steps = hidden // tile
     in_specs = [resident((quarter, width))] * 4 + [
         pl.BlockSpec((None, 6, width), lambda s, me: (v, 0, 0), pipeline_mode=pl.Buffered(1)),
-        pl.BlockSpec((heads, text, dim), lambda s, me: (0, v, 0), pipeline_mode=pl.Buffered(1)),
+        pl.BlockSpec((heads, text, k.shape[2]), lambda s, me: (0, v, 0), pipeline_mode=pl.Buffered(1)),
         pl.BlockSpec((heads, dim, text), lambda s, me: (0, 0, v), pipeline_mode=pl.Buffered(1)),
         pl.BlockSpec(memory_space=pl.ANY),
         pl.BlockSpec(memory_space=pl.ANY),
@@ -352,13 +377,17 @@
         in_specs=in_specs,
         out_specs=pl.BlockSpec((None, None, tokens, width), lambda s, me: (v, 0, 0, 0), pipeline_mode=pl.Buffered(1)),
         scratch_shapes=[
-            pltpu.VMEM((heads, dim, tokens), BF16),
+            pltpu.VMEM((heads, 128, tokens), BF16),
             pltpu.VMEM((total, tokens), BF16),
             pltpu.VMEM((tokens, width), BF16),
             pltpu.VMEM((tokens, width), BF16),
             pltpu.VMEM((tokens, width), F32),
             pltpu.VMEM((total, width), BF16),
             pltpu.VMEM((total, width), BF16),
+            pltpu.VMEM((text, 512), F32),
+            pltpu.VMEM((text, 512), F32),
+            pltpu.VMEM((text, 512), BF16),
+            pltpu.VMEM((text, 512), BF16),
             pltpu.SemaphoreType.DMA((2,)),
         ],
     )

time: 830 us -> 625 us (0.75)
  Pallas kernels: 801 us -> 597 us
    pallas_call x4, Pallas kernels: 381 us -> 266 us  [cross_mlp(): pl.pallas_call(functools.partial(cross_mlp_kernel, heads=heads, dim=dim),...]
    pallas_call x4, Pallas kernels: 286 us -> 197 us  [spatial(): pl.pallas_call(functools.partial(spatial_kernel, heads=heads, dim=dim), g...]
  transfers between devices with their start and end apart: 24 -> 24, of which waited for: 0 -> 0; matrix products, arithmetic and copies ran while one was open for 0% -> 0% of each run, Pallas kernels for 77% -> 78%
where the time goes in v2:
time: 625 us; the launch traced here: 619 us
  Pallas kernels  597 us (96%)
  starting transfers between devices  18.3 us (3%)
    pallas_call x4, Pallas kernels, cross_mlp(): pl.pallas_call(functools.partial(cross_mlp_kernel, heads=heads, dim=dim),...  266 us
    pallas_call x4, Pallas kernels, spatial(): pl.pallas_call(functools.partial(spatial_kernel, heads=heads, dim=dim), g...  197 us
    pallas_call x4, Pallas kernels, temporal(): pl.pallas_call(functools.partial(temporal_kernel, heads=heads, dim=dim),...  121 us
    ppermute x24, starting transfers between devices, swap(): lax.ppermute(parts[d], 'sp', [(i, i ^ d) for i in range(devices)])  18.3 us
    pallas_call x1, Pallas kernels, text_kv(): pl.pallas_call(functools.partial(text_kernel, heads=heads, dim=dim), grid...  13.9 us
  transfers between devices with their start and end apart: 24, of which 0 were waited for; matrix products, arithmetic and copies ran while one was open for 0% of the time, Pallas kernels for 78%

profile of v2, /device:TPU:0, one launch (start us, length us, event | category | flops | bytes accessed | tf_op | source)
XLA Modules:
  0.0 618.8 jit_solution(5614616399807017882)
XLA Ops:
  0.0 1.6 copy.17.mod_ref
  1.6 49.0 %spatial.7 = (bf16[256,1408]{1,0:T(8,128)(2,1)}, bf16[256,1408]{1,0:T(8,128)(2,1)}, bf16[256,1408]{1,0:T(8,128)(2,1)}, bf16[256,1408]{1,0:T(8,128)(2,1)}) custom-call(s32[1]{0:T(128)} %bitcast.me_ref, bf16[4,1,1024,1408]{3,2,1,0:T(8,128)(2,1)} %x_ref.7, f32[4,6,1408]{2,1,0:T(8,128)} %copy.17.mod_ref, bf16[3,1408,1408]{2,1,0:T(8,128)(2,1)} %bitcast.9, ...), custom_call_target="tpu_custom_call" | custom-call | flops 22145925120 | bytes 21626880 | tf_op jit(solution)/shard_map/spatial/pallas_call | solution.py:285
  50.6 0.8 collective-permute-start.18
  51.3 2.5 collective-permute-start.19
  53.9 0.1 collective-permute-start.20
  53.9 49.1 %spatial.6 = (bf16[256,1408]{1,0:T(8,128)(2,1)}, bf16[256,1408]{1,0:T(8,128)(2,1)}, bf16[256,1408]{1,0:T(8,128)(2,1)}, bf16[256,1408]{1,0:T(8,128)(2,1)}) custom-call(s32[1]{0:T(128)} %bitcast.me_ref, bf16[4,1,1024,1408]{3,2,1,0:T(8,128)(2,1)} %x_ref.7, f32[4,6,1408]{2,1,0:T(8,128)} %copy.17.mod_ref, bf16[3,1408,1408]{2,1,0:T(8,128)(2,1)} %bitcast.10, ...), custom_call_target="tpu_custom_call" | custom-call | flops 22145925120 | bytes 21626880 | tf_op jit(solution)/shard_map/spatial/pallas_call | solution.py:285
  103.1 0.2 collective-permute-start.12
  103.3 2.0 collective-permute-start.13
  105.2 49.4 %spatial.5 = (bf16[256,1408]{1,0:T(8,128)(2,1)}, bf16[256,1408]{1,0:T(8,128)(2,1)}, bf16[256,1408]{1,0:T(8,128)(2,1)}, bf16[256,1408]{1,0:T(8,128)(2,1)}) custom-call(s32[1]{0:T(128)} %bitcast.me_ref, bf16[4,1,1024,1408]{3,2,1,0:T(8,128)(2,1)} %x_ref.7, f32[4,6,1408]{2,1,0:T(8,128)} %copy.17.mod_ref, bf16[3,1408,1408]{2,1,0:T(8,128)(2,1)} %bitcast.11, ...), custom_call_target="tpu_custom_call" | custom-call | flops 22145925120 | bytes 21626880 | tf_op jit(solution)/shard_map/spatial/pallas_call | solution.py:285
  154.6 49.2 %spatial.4 = (bf16[256,1408]{1,0:T(8,128)(2,1)}, bf16[256,1408]{1,0:T(8,128)(2,1)}, bf16[256,1408]{1,0:T(8,128)(2,1)}, bf16[256,1408]{1,0:T(8,128)(2,1)}) custom-call(s32[1]{0:T(128)} %bitcast.me_ref, bf16[4,1,1024,1408]{3,2,1,0:T(8,128)(2,1)} %x_ref.7, f32[4,6,1408]{2,1,0:T(8,128)} %copy.17.mod_ref, bf16[3,1408,1408]{2,1,0:T(8,128)(2,1)} %bitcast.12, ...), custom_call_target="tpu_custom_call" | custom-call | flops 22145925120 | bytes 21626880 | tf_op jit(solution)/shard_map/spatial/pallas_call | solution.py:285
  203.8 0.0 copy-start.11
  203.8 13.9 %text_kv.1 = (bf16[16,1024,128]{2,1,0:T(8,128)(2,1)}, bf16[16,88,1024]{2,1,0:T(8,128)(2,1)}) custom-call(bf16[1024,1408]{1,0:T(8,128)(2,1)} %bitcast.34, bf16[2,1408,1408]{2,1,0:T(8,128)(2,1)} %bitcast.17), custom_call_target="tpu_custom_call" | custom-call | flops 8120172544 | bytes 16580608 | tf_op jit(solution)/shard_map/text_kv/pallas_call | solution.py:338
  217.6 0.0 collective-permute-done.18.x1
  217.6 0.0 collective-permute-start.14
  217.7 0.0 collective-permute-done.19.x2
  217.7 0.1 collective-permute-start.6
  217.8 0.0 collective-permute-done.20.x3
  217.8 2.0 collective-permute-start.7
  219.8 30.2 %temporal.7 = (bf16[256,1408]{1,0:T(8,128)(2,1)}, bf16[256,1408]{1,0:T(8,128)(2,1)}, bf16[256,1408]{1,0:T(8,128)(2,1)}, bf16[256,1408]{1,0:T(8,128)(2,1)}) custom-call(s32[1]{0:T(128)} %bitcast.me_ref, bf16[256,1408]{1,0:T(8,128)(2,1)} %get-tuple-element.65.x0, bf16[256,1408]{1,0:T(8,128)(2,1)} %copy-done.14, bf16[256,1408]{1,0:T(8,128)(2,1)} %copy-done.15, ...), custom_call_target="tpu_custom_call" | custom-call | flops 16240345088 | bytes 21626880 | tf_op jit(solution)/shard_map/temporal/pallas_call | solution.py:322
  250.0 0.0 collective-permute-done.12.x1
  250.0 0.5 collective-permute-start.8
  250.5 0.0 collective-permute-done.13.x2
  250.6 0.0 collective-permute-start
  250.6 0.0 collective-permute-done.14.x3
  250.6 1.6 collective-permute-start.1
  252.2 30.1 %temporal.6 = (bf16[256,1408]{1,0:T(8,128)(2,1)}, bf16[256,1408]{1,0:T(8,128)(2,1)}, bf16[256,1408]{1,0:T(8,128)(2,1)}, bf16[256,1408]{1,0:T(8,128)(2,1)}) custom-call(s32[1]{0:T(128)} %bitcast.me_ref, bf16[256,1408]{1,0:T(8,128)(2,1)} %get-tuple-element.57.x0, bf16[256,1408]{1,0:T(8,128)(2,1)} %copy-done.12, bf16[256,1408]{1,0:T(8,128)(2,1)} %copy-done.13, ...), custom_call_target="tpu_custom_call" | custom-call | flops 16240345088 | bytes 21626880 | tf_op jit(solution)/shard_map/temporal/pallas_call | solution.py:322
  282.4 0.0 collective-permute-done.6.x1
  282.4 0.5 collective-permute-start.2
  282.9 0.0 collective-permute-done.7.x2
  282.9 0.1 collective-permute-start.21
  283.0 0.0 collective-permute-done.8.x3
  283.0 1.6 collective-permute-start.22
  284.6 30.2 %temporal.5 = (bf16[256,1408]{1,0:T(8,128)(2,1)}, bf16[256,1408]{1,0:T(8,128)(2,1)}, bf16[256,1408]{1,0:T(8,128)(2,1)}, bf16[256,1408]{1,0:T(8,128)(2,1)}) custom-call(s32[1]{0:T(128)} %bitcast.me_ref, bf16[256,1408]{1,0:T(8,128)(2,1)} %get-tuple-element.49.x0, bf16[256,1408]{1,0:T(8,128)(2,1)} %collective-permute-done.6.x1, ...), custom_call_target="tpu_custom_call" | custom-call | flops 16240345088 | bytes 21626880 | tf_op jit(solution)/shard_map/temporal/pallas_call | solution.py:322
  314.8 0.0 collective-permute-done.x1
  314.8 0.2 collective-permute-start.23
  315.1 0.0 collective-permute-done.1.x2
  315.1 0.3 collective-permute-start.15
  315.4 0.0 collective-permute-done.2.x3
  315.4 1.6 collective-permute-start.16
  317.0 30.0 %temporal.4 = (bf16[256,1408]{1,0:T(8,128)(2,1)}, bf16[256,1408]{1,0:T(8,128)(2,1)}, bf16[256,1408]{1,0:T(8,128)(2,1)}, bf16[256,1408]{1,0:T(8,128)(2,1)}) custom-call(s32[1]{0:T(128)} %bitcast.me_ref, bf16[256,1408]{1,0:T(8,128)(2,1)} %get-tuple-element.39.x0, bf16[256,1408]{1,0:T(8,128)(2,1)} %collective-permute-done.x1, ...), custom_call_target="tpu_custom_call" | custom-call | flops 16240345088 | bytes 21626880 | tf_op jit(solution)/shard_map/temporal/pallas_call | solution.py:322
  347.1 0.0 collective-permute-done.21.x1
  347.1 0.0 collective-permute-start.17
  347.1 0.0 collective-permute-done.22.x2
  347.1 1.4 collective-permute-start.10
  348.5 0.0 collective-permute-done.23.x3
  348.5 0.5 collective-permute-start.11
  349.0 66.6 %cross_mlp.4.rest_0_ = bf16[4,1,1024,1408]{3,2,1,0:T(8,128)(2,1)} custom-call(s32[1]{0:T(128)} %bitcast.me_ref, bf16[256,1408]{1,0:T(8,128)(2,1)} %get-tuple-element.69.x0, bf16[256,1408]{1,0:T(8,128)(2,1)} %collective-permute-done.21.x1, bf16[256,1408]{1,0:T(8,128)(2,1)} %collective-permute-done.22.x2, bf16[256,1408]{1,0:T(8,128)(2,1)} %collective-permute-done.23.x3, ...), custom_call_target="tpu_custom_call" | custom-call | flops 42077257728 | bytes 45416448 | tf_op jit(solution)/shard_map/cross_mlp/pallas_call | solution.py:394
  415.6 0.0 collective-permute-done.15.x1
  415.6 0.3 collective-permute-start.9
  416.0 0.0 collective-permute-done.16.x2
  416.0 0.2 collective-permute-start.3
  416.2 0.0 collective-permute-done.17.x3
  416.2 1.6 collective-permute-start.4
  417.8 66.7 %cross_mlp.5.rest_0_ = bf16[4,1,1024,1408]{3,2,1,0:T(8,128)(2,1)} custom-call(s32[1]{0:T(128)} %bitcast.me_ref, bf16[256,1408]{1,0:T(8,128)(2,1)} %get-tuple-element.61.x0, bf16[256,1408]{1,0:T(8,128)(2,1)} %collective-permute-done.15.x1, bf16[256,1408]{1,0:T(8,128)(2,1)} %collective-permute-done.16.x2, ...), custom_call_target="tpu_custom_call", output_to_operand_aliasing={{}: (12, {})} | custom-call | flops 42077257728 | bytes 45416448 | tf_op jit(solution)/shard_map/cross_mlp/pallas_call | solution.py:394
  484.5 0.0 collective-permute-done.10.x2
  484.5 0.1 collective-permute-start.5
  484.6 0.0 collective-permute-done.11.x3
  484.6 0.0 collective-permute-done.9.x1
  484.6 66.4 %cross_mlp.6.rest_0_ = bf16[4,1,1024,1408]{3,2,1,0:T(8,128)(2,1)} custom-call(s32[1]{0:T(128)} %bitcast.me_ref, bf16[256,1408]{1,0:T(8,128)(2,1)} %get-tuple-element.53.x0, bf16[256,1408]{1,0:T(8,128)(2,1)} %collective-permute-done.9.x1, bf16[256,1408]{1,0:T(8,128)(2,1)} %collective-permute-done.10.x2, ...), custom_call_target="tpu_custom_call", output_to_operand_aliasing={{}: (12, {})} | custom-call | flops 42077257728 | bytes 45416448 | tf_op jit(solution)/shard_map/cross_mlp/pallas_call | solution.py:394
  551.0 0.0 collective-permute-done.3.x1
  551.0 0.0 collective-permute-done.4.x2
  551.0 0.0 collective-permute-done.5.x3
  551.0 0.9 copy-done.16
  552.0 66.4 %cross_mlp.7 = bf16[4,1,1024,1408]{3,2,1,0:T(8,128)(2,1)} custom-call(s32[1]{0:T(128)} %bitcast.me_ref, bf16[256,1408]{1,0:T(8,128)(2,1)} %get-tuple-element.43.x0, bf16[256,1408]{1,0:T(8,128)(2,1)} %collective-permute-done.3.x1, bf16[256,1408]{1,0:T(8,128)(2,1)} %copy-done.16, ...), custom_call_target="tpu_custom_call", output_to_operand_aliasing={{}: (12, {})} | custom-call | flops 42077257728 | bytes 45416448 | tf_op jit(solution)/shard_map/cross_mlp/pallas_call | solution.py:394
  (32 shorter events, 0.1 us)
Async XLA Ops:
  50.6 167.0 %collective-permute-start.18 = (bf16[256,1408]{1,0:T(8,128)(2,1)}, bf16[256,1408]{1,0:T(8,128)(2,1)S(1)}, u32[]{:S(2)}, u32[]{:S(2)}) collective-permute-start(bf16[256,1408]{1,0:T(8,128)(2,1)} %get-tuple-element.66), channel_id=1, source_target_pairs={{0,1},{1,0},{2,3},{3,2},{4,5},{5,4},{6,7},{7,6},{8,9},{9,8},{10,11... | collective-permute-start | bytes 2162696 | tf_op jit(solution)/shard_map/ppermute | solution.py:406
  51.3 166.3 %collective-permute-start.19 = (bf16[256,1408]{1,0:T(8,128)(2,1)}, bf16[256,1408]{1,0:T(8,128)(2,1)S(1)}, u32[]{:S(2)}, u32[]{:S(2)}) collective-permute-start(bf16[256,1408]{1,0:T(8,128)(2,1)} %get-tuple-element.67), channel_id=1, source_target_pairs={{0,2},{1,3},{2,0},{3,1},{4,6},{5,7},{6,4},{7,5},{8,10},{9,11},{10,... | collective-permute-start | bytes 2162696 | tf_op jit(solution)/shard_map/ppermute | solution.py:406
  53.9 164.0 %collective-permute-start.20 = (bf16[256,1408]{1,0:T(8,128)(2,1)}, bf16[256,1408]{1,0:T(8,128)(2,1)}, u32[]{:S(2)}, u32[]{:S(2)}) collective-permute-start(bf16[256,1408]{1,0:T(8,128)(2,1)} %get-tuple-element.68), channel_id=1, source_target_pairs={{0,3},{1,2},{2,1},{3,0},{4,7},{5,6},{6,5},{7,4},{8,11},{9,10},{10,... | collective-permute-start | bytes 2162696 | tf_op jit(solution)/shard_map/ppermute | solution.py:406
  103.1 146.9 %collective-permute-start.12 = (bf16[256,1408]{1,0:T(8,128)(2,1)}, bf16[256,1408]{1,0:T(8,128)(2,1)S(1)}, u32[]{:S(2)}, u32[]{:S(2)}) collective-permute-start(bf16[256,1408]{1,0:T(8,128)(2,1)} %get-tuple-element.58), channel_id=1, source_target_pairs={{0,1},{1,0},{2,3},{3,2},{4,5},{5,4},{6,7},{7,6},{8,9},{9,8},{10,11... | collective-permute-start | bytes 2162696 | tf_op jit(solution)/shard_map/ppermute | solution.py:406
  103.3 147.3 %collective-permute-start.13 = (bf16[256,1408]{1,0:T(8,128)(2,1)}, bf16[256,1408]{1,0:T(8,128)(2,1)S(1)}, u32[]{:S(2)}, u32[]{:S(2)}) collective-permute-start(bf16[256,1408]{1,0:T(8,128)(2,1)} %get-tuple-element.59), channel_id=1, source_target_pairs={{0,2},{1,3},{2,0},{3,1},{4,6},{5,7},{6,4},{7,5},{8,10},{9,11},{10,... | collective-permute-start | bytes 2162696 | tf_op jit(solution)/shard_map/ppermute | solution.py:406
  203.8 14.1 %copy-start.11 = (bf16[256,1408]{1,0:T(8,128)(2,1)S(1)}, bf16[256,1408]{1,0:T(8,128)(2,1)}, u32[]{:S(2)}) copy-start(bf16[256,1408]{1,0:T(8,128)(2,1)} %get-tuple-element.51) | copy-start | bytes 2162692
  217.6 2.2 copy-start.14
  217.6 32.9 %collective-permute-start.14 = (bf16[256,1408]{1,0:T(8,128)(2,1)}, bf16[256,1408]{1,0:T(8,128)(2,1)}, u32[]{:S(2)}, u32[]{:S(2)}) collective-permute-start(bf16[256,1408]{1,0:T(8,128)(2,1)} %get-tuple-element.60), channel_id=1, source_target_pairs={{0,3},{1,2},{2,1},{3,0},{4,7},{5,6},{6,5},{7,4},{8,11},{9,10},{10,... | collective-permute-start | bytes 2162696 | tf_op jit(solution)/shard_map/ppermute | solution.py:406
  217.7 2.1 copy-start.15
  217.7 64.7 %collective-permute-start.6 = (bf16[256,1408]{1,0:T(8,128)(2,1)}, bf16[256,1408]{1,0:T(8,128)(2,1)}, u32[]{:S(2)}, u32[]{:S(2)}) collective-permute-start(bf16[256,1408]{1,0:T(8,128)(2,1)} %get-tuple-element.50), channel_id=1, source_target_pairs={{0,1},{1,0},{2,3},{3,2},{4,5},{5,4},{6,7},{7,6},{8,9},{9,8},{10,11... | collective-permute-start | bytes 2162696 | tf_op jit(solution)/shard_map/ppermute | solution.py:406
  217.8 65.1 %collective-permute-start.7 = (bf16[256,1408]{1,0:T(8,128)(2,1)S(1)}, bf16[256,1408]{1,0:T(8,128)(2,1)}, u32[]{:S(2)}, u32[]{:S(2)}) collective-permute-start(bf16[256,1408]{1,0:T(8,128)(2,1)S(1)} %copy-done.11), channel_id=1, source_target_pairs={{0,2},{1,3},{2,0},{3,1},{4,6},{5,7},{6,4},{7,5},{8,10},{9,11},{10,... | collective-permute-start | bytes 2162696 | tf_op jit(solution)/shard_map/ppermute | solution.py:406
  219.8 30.2 %copy-start.10 = (bf16[256,1408]{1,0:T(8,128)(2,1)S(1)}, bf16[256,1408]{1,0:T(8,128)(2,1)}, u32[]{:S(2)}) copy-start(bf16[256,1408]{1,0:T(8,128)(2,1)} %get-tuple-element.52) | copy-start | bytes 2162692
  219.8 30.8 %copy-start.4 = (bf16[256,1408]{1,0:T(8,128)(2,1)S(1)}, bf16[256,1408]{1,0:T(8,128)(2,1)}, u32[]{:S(2)}) copy-start(bf16[256,1408]{1,0:T(8,128)(2,1)} %get-tuple-element.41) | copy-start | bytes 2162692
  250.0 2.2 copy-start.12
  250.0 33.0 %collective-permute-start.8 = (bf16[256,1408]{1,0:T(8,128)(2,1)S(1)}, bf16[256,1408]{1,0:T(8,128)(2,1)}, u32[]{:S(2)}, u32[]{:S(2)}) collective-permute-start(bf16[256,1408]{1,0:T(8,128)(2,1)S(1)} %copy-done.10), channel_id=1, source_target_pairs={{0,3},{1,2},{2,1},{3,0},{4,7},{5,6},{6,5},{7,4},{8,11},{9,10},{10,... | collective-permute-start | bytes 2162696 | tf_op jit(solution)/shard_map/ppermute | solution.py:406
  250.6 1.7 copy-start.13
  250.6 64.3 %collective-permute-start = (bf16[256,1408]{1,0:T(8,128)(2,1)}, bf16[256,1408]{1,0:T(8,128)(2,1)}, u32[]{:S(2)}, u32[]{:S(2)}) collective-permute-start(bf16[256,1408]{1,0:T(8,128)(2,1)} %get-tuple-element.40), channel_id=1, source_target_pairs={{0,1},{1,0},{2,3},{3,2},{4,5},{5,4},{6,7},{7,6},{8,9},{9,8},{10,11... | collective-permute-start | bytes 2162696 | tf_op jit(solution)/shard_map/ppermute | solution.py:406
  250.6 64.5 %collective-permute-start.1 = (bf16[256,1408]{1,0:T(8,128)(2,1)S(1)}, bf16[256,1408]{1,0:T(8,128)(2,1)}, u32[]{:S(2)}, u32[]{:S(2)}) collective-permute-start(bf16[256,1408]{1,0:T(8,128)(2,1)S(1)} %copy-done.4), channel_id=1, source_target_pairs={{0,2},{1,3},{2,0},{3,1},{4,6},{5,7},{6,4},{7,5},{8,10},{9,11},{10,... | collective-permute-start | bytes 2162696 | tf_op jit(solution)/shard_map/ppermute | solution.py:406
  252.2 30.2 %copy-start.1 = (bf16[256,1408]{1,0:T(8,128)(2,1)S(1)}, bf16[256,1408]{1,0:T(8,128)(2,1)}, u32[]{:S(2)}) copy-start(bf16[256,1408]{1,0:T(8,128)(2,1)} %get-tuple-element.42) | copy-start | bytes 2162692
  252.2 30.8 %copy-start.3 = (bf16[256,1408]{1,0:T(8,128)(2,1)S(1)}, bf16[256,1408]{1,0:T(8,128)(2,1)}, u32[]{:S(2)}) copy-start(bf16[256,1408]{1,0:T(8,128)(2,1)} %get-tuple-element.71) | copy-start | bytes 2162692
  282.4 33.0 %collective-permute-start.2 = (bf16[256,1408]{1,0:T(8,128)(2,1)S(1)}, bf16[256,1408]{1,0:T(8,128)(2,1)}, u32[]{:S(2)}, u32[]{:S(2)}) collective-permute-start(bf16[256,1408]{1,0:T(8,128)(2,1)S(1)} %copy-done.1), channel_id=1, source_target_pairs={{0,3},{1,2},{2,1},{3,0},{4,7},{5,6},{6,5},{7,4},{8,11},{9,10},{10,... | collective-permute-start | bytes 2162696 | tf_op jit(solution)/shard_map/ppermute | solution.py:406
  282.9 64.1 %collective-permute-start.21 = (bf16[256,1408]{1,0:T(8,128)(2,1)}, bf16[256,1408]{1,0:T(8,128)(2,1)}, u32[]{:S(2)}, u32[]{:S(2)}) collective-permute-start(bf16[256,1408]{1,0:T(8,128)(2,1)} %get-tuple-element.70), channel_id=1, source_target_pairs={{0,1},{1,0},{2,3},{3,2},{4,5},{5,4},{6,7},{7,6},{8,9},{9,8},{10,11... | collective-permute-start | bytes 2162696 | tf_op jit(solution)/shard_map/ppermute | solution.py:406
  283.0 64.1 %collective-permute-start.22 = (bf16[256,1408]{1,0:T(8,128)(2,1)S(1)}, bf16[256,1408]{1,0:T(8,128)(2,1)}, u32[]{:S(2)}, u32[]{:S(2)}) collective-permute-start(bf16[256,1408]{1,0:T(8,128)(2,1)S(1)} %copy-done.3), channel_id=1, source_target_pairs={{0,2},{1,3},{2,0},{3,1},{4,6},{5,7},{6,4},{7,5},{8,10},{9,11},{10,... | collective-permute-start | bytes 2162696 | tf_op jit(solution)/shard_map/ppermute | solution.py:406
  284.6 30.2 %copy-start = (bf16[256,1408]{1,0:T(8,128)(2,1)S(1)}, bf16[256,1408]{1,0:T(8,128)(2,1)}, u32[]{:S(2)}) copy-start(bf16[256,1408]{1,0:T(8,128)(2,1)} %get-tuple-element.72) | copy-start | bytes 2162692
  284.6 30.8 %copy-start.5 = (bf16[256,1408]{1,0:T(8,128)(2,1)S(1)}, bf16[256,1408]{1,0:T(8,128)(2,1)}, u32[]{:S(2)}) copy-start(bf16[256,1408]{1,0:T(8,128)(2,1)} %get-tuple-element.63) | copy-start | bytes 2162692
  314.8 33.7 %collective-permute-start.23 = (bf16[256,1408]{1,0:T(8,128)(2,1)S(1)}, bf16[256,1408]{1,0:T(8,128)(2,1)}, u32[]{:S(2)}, u32[]{:S(2)}) collective-permute-start(bf16[256,1408]{1,0:T(8,128)(2,1)S(1)} %copy-done), channel_id=1, source_target_pairs={{0,3},{1,2},{2,1},{3,0},{4,7},{5,6},{6,5},{7,4},{8,11},{9,10},{10,... | collective-permute-start | bytes 2162696 | tf_op jit(solution)/shard_map/ppermute | solution.py:406
  315.1 100.5 %collective-permute-start.15 = (bf16[256,1408]{1,0:T(8,128)(2,1)}, bf16[256,1408]{1,0:T(8,128)(2,1)}, u32[]{:S(2)}, u32[]{:S(2)}) collective-permute-start(bf16[256,1408]{1,0:T(8,128)(2,1)} %get-tuple-element.62), channel_id=1, source_target_pairs={{0,1},{1,0},{2,3},{3,2},{4,5},{5,4},{6,7},{7,6},{8,9},{9,8},{10,11... | collective-permute-start | bytes 2162696 | tf_op jit(solution)/shard_map/ppermute | solution.py:406
  315.4 100.5 %collective-permute-start.16 = (bf16[256,1408]{1,0:T(8,128)(2,1)S(1)}, bf16[256,1408]{1,0:T(8,128)(2,1)}, u32[]{:S(2)}, u32[]{:S(2)}) collective-permute-start(bf16[256,1408]{1,0:T(8,128)(2,1)S(1)} %copy-done.5), channel_id=1, source_target_pairs={{0,2},{1,3},{2,0},{3,1},{4,6},{5,7},{6,4},{7,5},{8,10},{9,11},{10,... | collective-permute-start | bytes 2162696 | tf_op jit(solution)/shard_map/ppermute | solution.py:406
  317.0 30.0 %copy-start.2 = (bf16[256,1408]{1,0:T(8,128)(2,1)S(1)}, bf16[256,1408]{1,0:T(8,128)(2,1)}, u32[]{:S(2)}) copy-start(bf16[256,1408]{1,0:T(8,128)(2,1)} %get-tuple-element.64) | copy-start | bytes 2162692
  317.0 31.5 %copy-start.7 = (bf16[256,1408]{1,0:T(8,128)(2,1)S(1)}, bf16[256,1408]{1,0:T(8,128)(2,1)}, u32[]{:S(2)}) copy-start(bf16[256,1408]{1,0:T(8,128)(2,1)} %get-tuple-element.56) | copy-start | bytes 2162692
  347.1 69.1 %collective-permute-start.17 = (bf16[256,1408]{1,0:T(8,128)(2,1)S(1)}, bf16[256,1408]{1,0:T(8,128)(2,1)}, u32[]{:S(2)}, u32[]{:S(2)}) collective-permute-start(bf16[256,1408]{1,0:T(8,128)(2,1)S(1)} %copy-done.2), channel_id=1, source_target_pairs={{0,3},{1,2},{2,1},{3,0},{4,7},{5,6},{6,5},{7,4},{8,11},{9,10},{10,... | collective-permute-start | bytes 2162696 | tf_op jit(solution)/shard_map/ppermute | solution.py:406
  347.1 137.3 %collective-permute-start.10 = (bf16[256,1408]{1,0:T(8,128)(2,1)}, bf16[256,1408]{1,0:T(8,128)(2,1)}, u32[]{:S(2)}, u32[]{:S(2)}) collective-permute-start(bf16[256,1408]{1,0:T(8,128)(2,1)} %get-tuple-element.55), channel_id=1, source_target_pairs={{0,2},{1,3},{2,0},{3,1},{4,6},{5,7},{6,4},{7,5},{8,10},{9,11},{10,... | collective-permute-start | bytes 2162696 | tf_op jit(solution)/shard_map/ppermute | solution.py:406
  348.5 136.1 %collective-permute-start.11 = (bf16[256,1408]{1,0:T(8,128)(2,1)S(1)}, bf16[256,1408]{1,0:T(8,128)(2,1)}, u32[]{:S(2)}, u32[]{:S(2)}) collective-permute-start(bf16[256,1408]{1,0:T(8,128)(2,1)S(1)} %copy-done.7), channel_id=1, source_target_pairs={{0,3},{1,2},{2,1},{3,0},{4,7},{5,6},{6,5},{7,4},{8,11},{9,10},{10,... | collective-permute-start | bytes 2162696 | tf_op jit(solution)/shard_map/ppermute | solution.py:406
  349.0 66.6 %copy-start.6 = (bf16[256,1408]{1,0:T(8,128)(2,1)S(1)}, bf16[256,1408]{1,0:T(8,128)(2,1)}, u32[]{:S(2)}) copy-start(bf16[256,1408]{1,0:T(8,128)(2,1)} %get-tuple-element.54) | copy-start | bytes 2162692
  349.0 67.2 %copy-start.9 = (bf16[256,1408]{1,0:T(8,128)(2,1)S(1)}, bf16[256,1408]{1,0:T(8,128)(2,1)}, u32[]{:S(2)}) copy-start(bf16[256,1408]{1,0:T(8,128)(2,1)} %get-tuple-element.45) | copy-start | bytes 2162692
  415.6 69.0 %collective-permute-start.9 = (bf16[256,1408]{1,0:T(8,128)(2,1)S(1)}, bf16[256,1408]{1,0:T(8,128)(2,1)}, u32[]{:S(2)}, u32[]{:S(2)}) collective-permute-start(bf16[256,1408]{1,0:T(8,128)(2,1)S(1)} %copy-done.6), channel_id=1, source_target_pairs={{0,1},{1,0},{2,3},{3,2},{4,5},{5,4},{6,7},{7,6},{8,9},{9,8},{10,11... | collective-permute-start | bytes 2162696 | tf_op jit(solution)/shard_map/ppermute | solution.py:406
  416.0 135.0 %collective-permute-start.3 = (bf16[256,1408]{1,0:T(8,128)(2,1)}, bf16[256,1408]{1,0:T(8,128)(2,1)}, u32[]{:S(2)}, u32[]{:S(2)}) collective-permute-start(bf16[256,1408]{1,0:T(8,128)(2,1)} %get-tuple-element.44), channel_id=1, source_target_pairs={{0,1},{1,0},{2,3},{3,2},{4,5},{5,4},{6,7},{7,6},{8,9},{9,8},{10,11... | collective-permute-start | bytes 2162696 | tf_op jit(solution)/shard_map/ppermute | solution.py:406
  416.2 134.8 %collective-permute-start.4 = (bf16[256,1408]{1,0:T(8,128)(2,1)S(1)}, bf16[256,1408]{1,0:T(8,128)(2,1)S(1)}, u32[]{:S(2)}, u32[]{:S(2)}) collective-permute-start(bf16[256,1408]{1,0:T(8,128)(2,1)S(1)} %copy-done.9), channel_id=1, source_target_pairs={{0,2},{1,3},{2,0},{3,1},{4,6},{5,7},{6,4},{7,5},{8,10},{9,11},{10,... | collective-permute-start | bytes 2162696 | tf_op jit(solution)/shard_map/ppermute | solution.py:406
  417.8 66.7 %copy-start.8 = (bf16[256,1408]{1,0:T(8,128)(2,1)S(1)}, bf16[256,1408]{1,0:T(8,128)(2,1)}, u32[]{:S(2)}) copy-start(bf16[256,1408]{1,0:T(8,128)(2,1)} %get-tuple-element.46) | copy-start | bytes 2162692
  484.5 66.5 %collective-permute-start.5 = (bf16[256,1408]{1,0:T(8,128)(2,1)S(1)}, bf16[256,1408]{1,0:T(8,128)(2,1)}, u32[]{:S(2)}, u32[]{:S(2)}) collective-permute-start(bf16[256,1408]{1,0:T(8,128)(2,1)S(1)} %copy-done.8), channel_id=1, source_target_pairs={{0,3},{1,2},{2,1},{3,0},{4,7},{5,6},{6,5},{7,4},{8,11},{9,10},{10,... | collective-permute-start | bytes 2162696 | tf_op jit(solution)/shard_map/ppermute | solution.py:406
  551.0 0.9 copy-start.16

commit v3 on v2

v3 whole, which is shorter than its diff:
```python
import functools

import jax
import jax.numpy as jnp
from jax import lax
from jax.experimental import pallas as pl
from jax.experimental.pallas import tpu as pltpu
from jax.sharding import PartitionSpec as P

LN_EPS = 1e-6
LOG2E = 1.4426950408889634
VMEM_LIMIT = 60 * 1024 * 1024
NT = (((1,), (1,)), ((), ()))
TN = (((0,), (0,)), ((), ()))
F32 = jnp.float32
BF16 = jnp.bfloat16


def dot(lhs, rhs, dims=(((1,), (0,)), ((), ()))):
    return lax.dot_general(lhs, rhs, dims, preferred_element_type=F32)


def normed_rows(rows, shift, scale):
    rows = rows.astype(F32)
    centered = rows - jnp.mean(rows, axis=-1, keepdims=True)
    unit = centered * lax.rsqrt(jnp.mean(centered * centered, axis=-1, keepdims=True) + LN_EPS)
    return (unit * (1.0 + scale) + shift).astype(BF16)


def resident(shape):
    return pl.BlockSpec(shape, lambda *_: (0,) * len(shape), pipeline_mode=pl.Buffered(1))


def project_heads(w_ref, acts, q_s, k_s, v_s, heads, dim, cols):
    chunk = cols.stop - cols.start
    part = acts[cols, :]
    q_s[:, :dim, cols] = dot(w_ref[0], part, NT).reshape(heads, dim, chunk).astype(BF16)
    v_s[:, :, cols] = dot(w_ref[2], part, NT).reshape(heads, dim, chunk).astype(BF16)
    k_t = dot(w_ref[1], part, NT)
    for h in range(heads):
        k_s[h, cols, :dim] = k_t[h * dim:(h + 1) * dim].T.astype(BF16)


def attend_heads(q, k, v, out, scores, probs, base, row, scale, count, block):
    tokens, keys, dim = out.shape[1], k.shape[1], v.shape[1]
    chunk = min(256, keys)
    blocks = [(h, c) for c in range(tokens // block) for h in range(count)]
    tops, mixed = {}, {}

    def score(n):
        h, c = blocks[n]
        top = None
        for r in range(0, keys, chunk):
            s = dot(k[base + h, r:r + chunk, :], q[base + h, :, c * block:(c + 1) * block])
            scores[n % 2][r:r + chunk, :] = s
            part = jnp.max(s.reshape(chunk // 8, 8, block), axis=0)
            top = part if top is None else jnp.maximum(top, part)
        tops[n] = jnp.max(top, axis=0, keepdims=True)

    def mix(n):
        h, c = blocks[n]
        total = None
        for r in range(0, keys, chunk):
            p = jnp.exp2((scores[n % 2][r:r + chunk, :] - tops[n]) * scale)
            part = jnp.sum(p.reshape(chunk // 8, 8, block), axis=0)
            total = part if total is None else total + part
            probs[n % 2][r:r + chunk, :] = p.astype(BF16)
        mixed[h] = dot(v[base + h], probs[n % 2][...]) / jnp.sum(total, axis=0, keepdims=True)
        if h == count - 1:
            out[pl.ds(row, count * dim), c * block:(c + 1) * block] = jnp.concatenate([mixed[i] for i in range(count)], axis=0).astype(BF16)

    score(0)
    for n in range(len(blocks)):
        if n + 1 < len(blocks):
            score(n + 1)
        mix(n)


def gelu(x):
    return x * (0.5 + 0.5 * jnp.tanh(x * (0.7978845608028654 + 0.7978845608028654 * 0.044715 * (x * x))))


def spatial_kernel(me_ref, x_ref, mod_ref, w_ref, wo_hbm, o0, o1, o2, o3, u_s, q_s, k_s, v_s, a_s, wo_s, s0, s1, p0, p1, sem, *, heads, dim):
    v, g = pl.program_id(0), pl.program_id(1)
    tokens = x_ref.shape[0]
    quarter = tokens // 4
    halves = (slice(0, tokens // 2), slice(tokens // 2, tokens))
    wo_copy = pltpu.make_async_copy(wo_hbm, wo_s, sem)
    scale = dim ** -0.5 * LOG2E

    @pl.when((v == 0) & (g == 0))
    def _():
        q_s[:, dim:, :] = jnp.zeros((heads, q_s.shape[1] - dim, tokens), BF16)
        k_s[:, :, dim:] = jnp.zeros((heads, tokens, k_s.shape[2] - dim), BF16)

    @pl.when(g == 0)
    def _():
        for rows in halves:
            u_s[rows, :] = normed_rows(x_ref[rows, :], mod_ref[0:1, :], mod_ref[1:2, :])
            project_heads(w_ref, u_s, q_s, k_s, v_s, heads, dim, rows)

    @pl.when(g > 0)
    def _():
        for rows in halves:
            project_heads(w_ref, u_s, q_s, k_s, v_s, heads, dim, rows)

    @pl.when((v == 0) & (g == 1))
    def _():
        wo_copy.start()

    def pair(i, carry):
        row = pl.multiple_of((g * heads + 2 * i) * dim, 2 * dim)
        attend_heads(q_s, k_s, v_s, a_s, (s0, s1), (p0, p1), 2 * i, row, scale, 2, 512)
        return carry

    lax.fori_loop(0, heads // 2, pair, 0)

    @pl.when((v == 0) & (g == pl.num_programs(1) - 1))
    def _():
        wo_copy.wait()

    @pl.when(g == pl.num_programs(1) - 1)
    def _():
        for d, o_ref in enumerate((o0, o1, o2, o3)):
            rows = pl.ds(pl.multiple_of(jnp.bitwise_xor(me_ref[0], d) * quarter, quarter), quarter)
            branch = dot(a_s[:, rows], wo_s[...], TN)
            o_ref[...] = (x_ref[rows, :].astype(F32) + mod_ref[2:3, :] * branch).astype(BF16)


def attend_frames(q_s, k_s, v_s, h, cols, quarter, scale):
    part = lambda ref, t: ref[h, :, t * quarter + cols:t * quarter + cols + 128].astype(F32)
    k = [part(k_s, t) for t in range(4)]
    v = [part(v_s, t) for t in range(4)]
    outs = []
    for t in range(4):
        q = part(q_s, t)
        s = [jnp.sum(q * one, axis=0, keepdims=True) for one in k]
        top = jnp.maximum(jnp.maximum(s[0], s[1]), jnp.maximum(s[2], s[3]))
        p = [jnp.exp2((one - top) * scale) for one in s]
        inv = 1.0 / (p[0] + p[1] + p[2] + p[3])
        p = [(one * inv).astype(BF16).astype(F32) for one in p]
        outs.append(p[0] * v[0] + p[1] * v[1] + p[2] * v[2] + p[3] * v[3])
    return outs


def temporal_kernel(me_ref, x0, x1, x2, x3, mod_ref, pos_ref, w_ref, wo_hbm, o0, o1, o2, o3, z_s, qa, ka, va, qb, kb, vb, a_s, wo_s, sem, *, heads, dim):
    v, g = pl.program_id(0), pl.program_id(1)
    quarter = x0.shape[0]
    frames = (x0, x1, x2, x3)
    group = heads * dim
    wo_copy = pltpu.make_async_copy(wo_hbm, wo_s, sem)
    scale = dim ** -0.5 * LOG2E

    def shift(d):
        pos = pos_ref[pl.ds(jnp.bitwise_xor(me_ref[0], d), 1), :]
        z_s[d * quarter:(d + 1) * quarter, :] = (frames[d][...].astype(F32) + pos).astype(BF16)

    def project(half, dsts, tokens):
        for j, dst in enumerate(dsts):
            part = dot(w_ref[j, half * group:(half + 1) * group, :], z_s[tokens, :], NT)
            dst[:, :, tokens] = part.reshape(heads, dim, 2 * quarter).astype(BF16)

    def attend(srcs, index):
        for i in range(heads // 2):
            rows = pl.ds(pl.multiple_of(index * group + 2 * i * dim, 2 * dim), 2 * dim)
            for cols in range(0, quarter, 128):
                first = attend_frames(*srcs, 2 * i, cols, quarter, scale)
                second = attend_frames(*srcs, 2 * i + 1, cols, quarter, scale)
                for t in range(4):
                    out = jnp.concatenate([first[t], second[t]], axis=0)
                    a_s[rows, t * quarter + cols:t * quarter + cols + 128] = out.astype(BF16)

    halves = (slice(0, 2 * quarter), slice(2 * quarter, 4 * quarter))
    first, second = (qa, ka, va), (qb, kb, vb)

    @pl.when(g == 0)
    def _():
        for d in range(4):
            shift(d)
        for tokens in halves:
            project(0, first, tokens)

    @pl.when(g > 0)
    def _():
        for tokens in halves:
            project(0, first, tokens)
        attend(second, 2 * g - 1)

    for tokens in halves:
        project(1, second, tokens)
    attend(first, 2 * g)

    @pl.when((v == 0) & (g == 0))
    def _():
        wo_copy.start()

    @pl.when((v == 0) & (g == pl.num_programs(1) - 1))
    def _():
        wo_copy.wait()

    @pl.when(g == pl.num_programs(1) - 1)
    def _():
        attend(second, 2 * g + 1)
        for d, (x, o_ref) in enumerate(zip(frames, (o0, o1, o2, o3))):
            branch = dot(a_s[:, d * quarter:(d + 1) * quarter], wo_s[...], TN)
            o_ref[...] = (x[...].astype(F32) + mod_ref[2:3, :] * branch).astype(BF16)


def text_kernel(t_ref, w_ref, k_ref, v_ref, *, heads, dim):
    tokens = t_ref.shape[0]
    k_t = dot(w_ref[0], t_ref[...], NT)
    v_ref[...] = dot(w_ref[1], t_ref[...], NT).reshape(heads, dim, tokens).astype(BF16)
    k_ref[:, :, dim:] = jnp.zeros((heads, tokens, k_ref.shape[2] - dim), BF16)
    for h in range(heads):
        k_ref[h, :, :dim] = k_t[h * dim:(h + 1) * dim].T.astype(BF16)


def cross_mlp_kernel(me_ref, x0, x1, x2, x3, mod_ref, k_ref, v_ref, wq_hbm, wo_hbm, w_in, w_out, *rest, heads, dim):
    y_ref, q_s, a_s, h_s, u_s, acc_s, wq_s, wo_s, s0, s1, p0, p1, sems = rest[-13:]
    v, step = pl.program_id(0), pl.program_id(1)
    quarter = x0.shape[0]
    tokens = 4 * quarter
    scale = dim ** -0.5 * LOG2E

    @pl.when(step == 0)
    def _():
        acc_s[...] = jnp.zeros_like(acc_s)

        @pl.when(v == 0)
        def _():
            pltpu.make_async_copy(wq_hbm, wq_s, sems.at[0]).start()
            pltpu.make_async_copy(wq_hbm, wq_s, sems.at[0]).wait()
            pltpu.make_async_copy(wo_hbm, wo_s, sems.at[1]).start()

        for d, x in enumerate((x0, x1, x2, x3)):
            cols = slice(d * quarter, (d + 1) * quarter)
            q_s[:, :dim, cols] = dot(wq_s[...], x[...], NT).reshape(heads, dim, quarter).astype(BF16)
        q_s[:, dim:, :] = jnp.zeros((heads, q_s.shape[1] - dim, tokens), BF16)

        def four(i, carry):
            row = pl.multiple_of(4 * i * dim, 4 * dim)
            attend_heads(q_s, k_ref, v_ref, a_s, (s0, s1), (p0, p1), 4 * i, row, scale, 4, 512)
            return carry

        lax.fori_loop(0, heads // 4, four, 0)

        @pl.when(v == 0)
        def _():
            pltpu.make_async_copy(wo_hbm, wo_s, sems.at[1]).wait()

        for d, x in enumerate((x0, x1, x2, x3)):
            rows = slice(d * quarter, (d + 1) * quarter)
            branch = dot(a_s[:, rows], wo_s[...], TN)
            after = (x[...].astype(F32) + branch).astype(BF16)
            h_s[rows, :] = after
            u_s[rows, :] = normed_rows(after, mod_ref[3:4, :], mod_ref[4:5, :])

    hidden = gelu(dot(u_s[...], w_in[...])).astype(BF16)
    acc_s[...] += dot(hidden, w_out[...])

    @pl.when(step == pl.num_programs(1) - 1)
    def _():
        for d in range(4):
            rows = slice(d * quarter, (d + 1) * quarter)
            dst = pl.ds(pl.multiple_of(jnp.bitwise_xor(me_ref[0], d) * quarter, quarter), quarter)
            y_ref[dst, :] = (h_s[rows, :].astype(F32) + mod_ref[5:6, :] * acc_s[rows, :]).astype(BF16)


def cost(flops, nbytes, exps=0):
    return pl.CostEstimate(flops=int(flops), bytes_accessed=int(nbytes), transcendentals=int(exps))


def params(axes=2):
    return pltpu.CompilerParams(dimension_semantics=("arbitrary",) * axes, vmem_limit_bytes=VMEM_LIMIT)


def spatial(me, latents, modulation, w_qkv, w_out, base, videos, heads):
    tokens, width = latents.shape[2:]
    dim = w_qkv.shape[2]
    total = w_qkv.shape[1] * dim
    group, quarter = heads * dim, tokens // 4
    spec = pltpu.PrefetchScalarGridSpec(
        num_scalar_prefetch=1,
        grid=(videos, w_qkv.shape[1] // heads),
        in_specs=[
            pl.BlockSpec((None, None, tokens, width), lambda v, g, me: (base + v, 0, 0, 0)),
            pl.BlockSpec((None, 6, width), lambda v, g, me: (base + v, 0, 0)),
            pl.BlockSpec((3, group, width), lambda v, g, me: (0, g, 0)),
            pl.BlockSpec(memory_space=pl.ANY),
        ],
        out_specs=[pl.BlockSpec((None, quarter, width), lambda v, g, me: (v, 0, 0))] * 4,
        scratch_shapes=[
            pltpu.VMEM((tokens, width), BF16),
            pltpu.VMEM((heads, 128, tokens), BF16),
            pltpu.VMEM((heads, tokens, 128), BF16),
            pltpu.VMEM((heads, dim, tokens), BF16),
            pltpu.VMEM((total, tokens), BF16),
            pltpu.VMEM((total, width), BF16),
            pltpu.VMEM((tokens, 512), F32),
            pltpu.VMEM((tokens, 512), F32),
            pltpu.VMEM((tokens, 512), BF16),
            pltpu.VMEM((tokens, 512), BF16),
            pltpu.SemaphoreType.DMA,
        ],
    )
    return pl.pallas_call(
        functools.partial(spatial_kernel, heads=heads, dim=dim),
        grid_spec=spec,
        out_shape=[jax.ShapeDtypeStruct((videos, quarter, width), BF16)] * 4,
        compiler_params=params(),
        cost_estimate=cost(videos * (8 * tokens * width * total + 4 * tokens * tokens * total), 2 * (4 * total * width + 2 * videos * tokens * width)),
        name="spatial",
    )(me, latents, modulation, w_qkv.reshape(3, total, width), w_out.reshape(total, width))


def temporal(me, frames, modulation, pos, w_qkv, w_out, base, heads):
    videos, quarter, width = frames[0].shape
    tokens = 4 * quarter
    dim = w_qkv.shape[2]
    total = w_qkv.shape[1] * dim
    group = heads * dim
    spec = pltpu.PrefetchScalarGridSpec(
        num_scalar_prefetch=1,
        grid=(videos, w_qkv.shape[1] // (2 * heads)),
        in_specs=[pl.BlockSpec((None, quarter, width), lambda v, g, me: (v, 0, 0))] * 4 + [
            pl.BlockSpec((None, 6, width), lambda v, g, me: (base + v, 0, 0)),
            resident(pos.shape),
            pl.BlockSpec((3, 2 * group, width), lambda v, g, me: (0, g, 0)),
            pl.BlockSpec(memory_space=pl.ANY),
        ],
        out_specs=[pl.BlockSpec((None, quarter, width), lambda v, g, me: (v, 0, 0))] * 4,
        scratch_shapes=[pltpu.VMEM((tokens, width), BF16)] + [pltpu.VMEM((heads, dim, tokens), BF16)] * 6 + [
            pltpu.VMEM((total, tokens), BF16),
            pltpu.VMEM((total, width), BF16),
            pltpu.SemaphoreType.DMA,
        ],
    )
    return pl.pallas_call(
        functools.partial(temporal_kernel, heads=heads, dim=dim),
        grid_spec=spec,
        out_shape=[jax.ShapeDtypeStruct((videos, quarter, width), BF16)] * 4,
        compiler_params=params(),
        cost_estimate=cost(videos * 8 * tokens * width * total, 2 * (4 * total * width + 2 * videos * tokens * width)),
        name="temporal",
    )(me, *frames, modulation, pos, w_qkv.reshape(3, total, width), w_out.reshape(total, width))


def text_kv(text, w_kv, heads):
    videos, length, width = text.shape
    dim = w_kv.shape[2]
    count = w_kv.shape[1]
    total = count * dim
    tokens = videos * length
    return pl.pallas_call(
        functools.partial(text_kernel, heads=heads, dim=dim),
        grid=(count // heads,),
        in_specs=[resident((tokens, width)), pl.BlockSpec((2, heads * dim, width), lambda g: (0, g, 0))],
        out_specs=[pl.BlockSpec((heads, tokens, 128), lambda g: (g, 0, 0)), pl.BlockSpec((heads, dim, tokens), lambda g: (g, 0, 0))],
        out_shape=[jax.ShapeDtypeStruct((count, tokens, 128), BF16), jax.ShapeDtypeStruct((count, dim, tokens), BF16)],
        compiler_params=params(1),
        cost_estimate=cost(4 * tokens * width * total, 2 * (2 * total * width + 3 * tokens * width)),
        name="text_kv",
    )(text.reshape(tokens, width), w_kv.reshape(2, total, width))


def cross_mlp(me, chunks, modulation, k, v_t, w_query, w_out_cross, w_in, w_out, base, y, videos):
    count, quarter, width = chunks[0].shape
    tokens = 4 * quarter
    heads, dim, all_text = v_t.shape
    text = all_text // videos
    total = heads * dim
    hidden = w_in.shape[1]
    tile = 512
    steps = hidden // tile
    in_specs = [pl.BlockSpec((None, quarter, width), lambda v, s, me: (v, 0, 0))] * 4 + [
        pl.BlockSpec((None, 6, width), lambda v, s, me: (base + v, 0, 0)),
        pl.BlockSpec((heads, text, k.shape[2]), lambda v, s, me: (0, base + v, 0)),
        pl.BlockSpec((heads, dim, text), lambda v, s, me: (0, 0, base + v)),
        pl.BlockSpec(memory_space=pl.ANY),
        pl.BlockSpec(memory_space=pl.ANY),
        pl.BlockSpec((width, tile), lambda v, s, me: (0, s)),
        pl.BlockSpec((tile, width), lambda v, s, me: (s, 0)),
    ]
    args = [me, *chunks, modulation, k, v_t, w_query.reshape(total, width), w_out_cross.reshape(total, width), w_in, w_out]
    aliases = {}
    if y is not None:
        in_specs.append(pl.BlockSpec(memory_space=pl.ANY))
        aliases = {len(args): 0}
        args.append(y)
    spec = pltpu.PrefetchScalarGridSpec(
        num_scalar_prefetch=1,
        grid=(count, steps),
        in_specs=in_specs,
        out_specs=pl.BlockSpec((None, None, tokens, width), lambda v, s, me: (base + v, 0, 0, 0)),
        scratch_shapes=[
            pltpu.VMEM((heads, 128, tokens), BF16),
            pltpu.VMEM((total, tokens), BF16),
            pltpu.VMEM((tokens, width), BF16),
            pltpu.VMEM((tokens, width), BF16),
            pltpu.VMEM((tokens, width), F32),
            pltpu.VMEM((total, width), BF16),
            pltpu.VMEM((total, width), BF16),
            pltpu.VMEM((text, 512), F32),
            pltpu.VMEM((text, 512), F32),
            pltpu.VMEM((text, 512), BF16),
            pltpu.VMEM((text, 512), BF16),
            pltpu.SemaphoreType.DMA((2,)),
        ],
    )
    return pl.pallas_call(
        functools.partial(cross_mlp_kernel, heads=heads, dim=dim),
        grid_spec=spec,
        out_shape=jax.ShapeDtypeStruct((videos, 1, tokens, width), BF16),
        input_output_aliases=aliases,
        compiler_params=params(),
        cost_estimate=cost(count * 4 * tokens * width * (hidden + total) + 4 * tokens * text * total, 4 * (width * hidden + total * width + tokens * width)),
        name="cross_mlp",
    )(*args)


def swap(parts, devices):
    return [parts[0]] + [lax.ppermute(parts[d], 'sp', [(i, i ^ d) for i in range(devices)]) for d in range(1, devices)]


def solution(mesh):
    act_spec = P('dp', 'sp', None, None)
    row_spec = P('dp', None, None)
    rep_two = P(None, None)
    rep_three = P(None, None, None)
    rep_four = P(None, None, None, None)
    in_specs = (act_spec, row_spec, row_spec, rep_two, rep_four, rep_three, rep_four, rep_three, rep_three, rep_four, rep_three, rep_two, rep_two)
    devices = mesh.shape['sp']

    def local_block(latents, text_ctx, modulation, pos_temporal, w_qkv_spatial, w_out_spatial, w_qkv_temporal, w_out_temporal, w_query_cross, w_kv_cross, w_out_cross, w_mlp_in, w_mlp_out):
        videos = latents.shape[0]
        me = lax.axis_index('sp').astype(jnp.int32).reshape(1)
        bases = range(0, videos, 2)
        by_patch = [swap(spatial(me, latents, modulation, w_qkv_spatial, w_out_spatial, b, 2, 4), devices) for b in bases]
        k, v_t = text_kv(text_ctx, w_kv_cross, 4)
        by_frame = [swap(temporal(me, by_patch[i], modulation, pos_temporal, w_qkv_temporal, w_out_temporal, b, 4), devices) for i, b in enumerate(bases)]
        y = None
        for i, b in enumerate(bases):
            y = cross_mlp(me, by_frame[i], modulation, k, v_t, w_query_cross, w_out_cross, w_mlp_in, w_mlp_out, b, y, videos)
        return y

    return jax.shard_map(local_block, mesh=mesh, in_specs=in_specs, out_specs=act_spec, check_vma=False)
```

time: 625 us -> 594 us (0.950)
  Pallas kernels: 597 us -> 564 us
  starting transfers between devices: 18.3 us -> 9.47 us
    pallas_call x4 -> x2, Pallas kernels: 197 us -> 178 us  [spatial(): pl.pallas_call(functools.partial(spatial_kernel, heads=heads, dim=dim), g...]
    pallas_call x4 -> x2, Pallas kernels: 266 us -> 254 us  [cross_mlp(): pl.pallas_call(functools.partial(cross_mlp_kernel, heads=heads, dim=dim),...]
    ppermute x24 -> x12, starting transfers between devices: 18.3 us -> 9.47 us  [swap(): lax.ppermute(parts[d], 'sp', [(i, i ^ d) for i in range(devices)])]
    pallas_call x4 -> x2, Pallas kernels: 121 us -> 119 us  [temporal(): pl.pallas_call(functools.partial(temporal_kernel, heads=heads, dim=dim),...]
  transfers between devices with their start and end apart: 24 -> 12, of which waited for: 0 -> 1; matrix products, arithmetic and copies ran while one was open for 0% -> 0% of each run, Pallas kernels for 78% -> 60%
where the time goes in v3:
time: 594 us; the launch traced here: 584 us
  Pallas kernels  564 us (95%)
  starting transfers between devices  9.47 us (2%)
    pallas_call x2, Pallas kernels, cross_mlp(): pl.pallas_call(functools.partial(cross_mlp_kernel, heads=heads, dim=dim),...  254 us
    pallas_call x2, Pallas kernels, spatial(): pl.pallas_call(functools.partial(spatial_kernel, heads=heads, dim=dim), g...  178 us
    pallas_call x2, Pallas kernels, temporal(): pl.pallas_call(functools.partial(temporal_kernel, heads=heads, dim=dim),...  119 us
    pallas_call x1, Pallas kernels, text_kv(): pl.pallas_call(functools.partial(text_kernel, heads=heads, dim=dim), grid...  13.8 us
  transfers between devices with their start and end apart: 12, of which 1 were waited for; matrix products, arithmetic and copies ran while one was open for 0% of the time, Pallas kernels for 60%

profile of v3, /device:TPU:0, one launch (start us, length us, event | category | flops | bytes accessed | tf_op | source)
XLA Modules:
  0.0 583.9 jit_solution(9318433636645246793)
XLA Ops:
  0.0 1.6 copy.15.mod_ref
  1.6 88.6 %spatial.3 = (bf16[2,256,1408]{2,1,0:T(8,128)(2,1)}, bf16[2,256,1408]{2,1,0:T(8,128)(2,1)}, bf16[2,256,1408]{2,1,0:T(8,128)(2,1)}, bf16[2,256,1408]{2,1,0:T(8,128)(2,1)}) custom-call(s32[1]{0:T(128)} %bitcast.me_ref, bf16[4,1,1024,1408]{3,2,1,0:T(8,128)(2,1)} %x_ref.3, f32[4,6,1408]{2,1,0:T(8,128)} %copy.15.mod_ref, bf16[3,1408,1408]{2,1,0:T(8,128)(2,1)} %bitcast.9, ...), custom_call_target="tpu_custom_call" | custom-call | flops 44291850240 | bytes 27394048 | tf_op jit(solution)/shard_map/spatial/pallas_call | solution.py:306
  90.3 0.8 collective-permute-start.6
  91.0 2.5 collective-permute-start.7
  93.5 0.1 collective-permute-start.8
  93.6 89.0 %spatial.2 = (bf16[2,256,1408]{2,1,0:T(8,128)(2,1)}, bf16[2,256,1408]{2,1,0:T(8,128)(2,1)}, bf16[2,256,1408]{2,1,0:T(8,128)(2,1)}, bf16[2,256,1408]{2,1,0:T(8,128)(2,1)}) custom-call(s32[1]{0:T(128)} %bitcast.me_ref, bf16[4,1,1024,1408]{3,2,1,0:T(8,128)(2,1)} %x_ref.3, f32[4,6,1408]{2,1,0:T(8,128)} %copy.15.mod_ref, bf16[3,1408,1408]{2,1,0:T(8,128)(2,1)} %bitcast.10, ...), custom_call_target="tpu_custom_call" | custom-call | flops 44291850240 | bytes 27394048 | tf_op jit(solution)/shard_map/spatial/pallas_call | solution.py:306
  182.6 0.2 collective-permute-start
  182.7 1.9 collective-permute-start.1
  184.7 13.8 %text_kv.1 = (bf16[16,1024,128]{2,1,0:T(8,128)(2,1)}, bf16[16,88,1024]{2,1,0:T(8,128)(2,1)}) custom-call(bf16[1024,1408]{1,0:T(8,128)(2,1)} %bitcast.22, bf16[2,1408,1408]{2,1,0:T(8,128)(2,1)} %bitcast.13), custom_call_target="tpu_custom_call" | custom-call | flops 8120172544 | bytes 16580608 | tf_op jit(solution)/shard_map/text_kv/pallas_call | solution.py:354
  198.4 0.0 collective-permute-done.6.x1
  198.4 0.0 collective-permute-start.2
  198.4 0.0 collective-permute-done.7.x2
  198.4 0.0 collective-permute-done.8.x3
  198.4 64.6 %temporal.3 = (bf16[2,256,1408]{2,1,0:T(8,128)(2,1)}, bf16[2,256,1408]{2,1,0:T(8,128)(2,1)}, bf16[2,256,1408]{2,1,0:T(8,128)(2,1)}, bf16[2,256,1408]{2,1,0:T(8,128)(2,1)}) custom-call(s32[1]{0:T(128)} %bitcast.me_ref, bf16[2,256,1408]{2,1,0:T(8,128)(2,1)} %get-tuple-element.33.x0, bf16[2,256,1408]{2,1,0:T(8,128)(2,1)} %collective-permute-done.6.x1, ...), custom_call_target="tpu_custom_call" | custom-call | flops 32480690176 | bytes 27394048 | tf_op jit(solution)/shard_map/temporal/pallas_call | solution.py:338
  263.1 0.2 collective-permute-start.9
  263.3 1.9 collective-permute-start.10
  265.2 0.0 collective-permute-done.x1
  265.2 0.0 copy-start
  265.2 0.0 collective-permute-start.11
  265.2 0.0 collective-permute-done.1.x2
  265.2 0.0 copy-start.1
  265.2 0.0 collective-permute-done.2.x3
  265.3 1.1 copy-done
  266.4 0.5 copy-done.1
  266.9 54.2 %temporal.2 = (bf16[2,256,1408]{2,1,0:T(8,128)(2,1)}, bf16[2,256,1408]{2,1,0:T(8,128)(2,1)}, bf16[2,256,1408]{2,1,0:T(8,128)(2,1)}, bf16[2,256,1408]{2,1,0:T(8,128)(2,1)}) custom-call(s32[1]{0:T(128)} %bitcast.me_ref, bf16[2,256,1408]{2,1,0:T(8,128)(2,1)} %get-tuple-element.23.x0, bf16[2,256,1408]{2,1,0:T(8,128)(2,1)} %copy-done, ...), custom_call_target="tpu_custom_call" | custom-call | flops 32480690176 | bytes 27394048 | tf_op jit(solution)/shard_map/temporal/pallas_call | solution.py:338
  321.0 0.0 collective-permute-start.3
  321.1 1.6 collective-permute-start.4
  322.7 0.0 collective-permute-done.9.x1
  322.7 0.2 collective-permute-start.5
  322.9 0.0 collective-permute-done.10.x2
  322.9 5.1 collective-permute-done.11.x3
  328.1 126.6 %cross_mlp.2.rest_0_ = bf16[4,1,1024,1408]{3,2,1,0:T(8,128)(2,1)} custom-call(s32[1]{0:T(128)} %bitcast.me_ref, bf16[2,256,1408]{2,1,0:T(8,128)(2,1)} %get-tuple-element.37.x0, bf16[2,256,1408]{2,1,0:T(8,128)(2,1)} %collective-permute-done.9.x1, bf16[2,256,1408]{2,1,0:T(8,128)(2,1)} %collective-permute-done.10.x2, ...), custom_call_target="tpu_custom_call" | custom-call | flops 82678120448 | bytes 45416448 | tf_op jit(solution)/shard_map/cross_mlp/pallas_call | solution.py:410
  454.7 0.0 collective-permute-done.3.x1
  454.7 0.0 copy-start.2
  454.7 0.0 collective-permute-done.4.x2
  454.8 0.0 copy-start.3
  454.8 0.0 collective-permute-done.5.x3
  454.8 1.1 copy-done.2
  455.8 0.5 copy-done.3
  456.4 127.2 %cross_mlp.3 = bf16[4,1,1024,1408]{3,2,1,0:T(8,128)(2,1)} custom-call(s32[1]{0:T(128)} %bitcast.me_ref, bf16[2,256,1408]{2,1,0:T(8,128)(2,1)} %get-tuple-element.27.x0, bf16[2,256,1408]{2,1,0:T(8,128)(2,1)} %copy-done.2, bf16[2,256,1408]{2,1,0:T(8,128)(2,1)} %copy-done.3, ...), custom_call_target="tpu_custom_call", output_to_operand_aliasing={{}: (12, {})} | custom-call | flops 82678120448 | bytes 45416448 | tf_op jit(solution)/shard_map/cross_mlp/pallas_call | solution.py:410
Async XLA Ops:
  90.3 108.2 %collective-permute-start.6 = (bf16[2,256,1408]{2,1,0:T(8,128)(2,1)}, bf16[2,256,1408]{2,1,0:T(8,128)(2,1)}, u32[]{:S(2)}, u32[]{:S(2)}) collective-permute-start(bf16[2,256,1408]{2,1,0:T(8,128)(2,1)} %get-tuple-element.34), channel_id=1, source_target_pairs={{0,1},{1,0},{2,3},{3,2},{4,5},{5,4},{6,7},{7,6},{8,9},{9,8},{10,11... | collective-permute-start | bytes 4325384 | tf_op jit(solution)/shard_map/ppermute | solution.py:422
  91.0 107.4 %collective-permute-start.7 = (bf16[2,256,1408]{2,1,0:T(8,128)(2,1)}, bf16[2,256,1408]{2,1,0:T(8,128)(2,1)}, u32[]{:S(2)}, u32[]{:S(2)}) collective-permute-start(bf16[2,256,1408]{2,1,0:T(8,128)(2,1)} %get-tuple-element.35), channel_id=1, source_target_pairs={{0,2},{1,3},{2,0},{3,1},{4,6},{5,7},{6,4},{7,5},{8,10},{9,11},{10,... | collective-permute-start | bytes 4325384 | tf_op jit(solution)/shard_map/ppermute | solution.py:422
  93.5 104.9 %collective-permute-start.8 = (bf16[2,256,1408]{2,1,0:T(8,128)(2,1)}, bf16[2,256,1408]{2,1,0:T(8,128)(2,1)}, u32[]{:S(2)}, u32[]{:S(2)}) collective-permute-start(bf16[2,256,1408]{2,1,0:T(8,128)(2,1)} %get-tuple-element.36), channel_id=1, source_target_pairs={{0,3},{1,2},{2,1},{3,0},{4,7},{5,6},{6,5},{7,4},{8,11},{9,10},{10,... | collective-permute-start | bytes 4325384 | tf_op jit(solution)/shard_map/ppermute | solution.py:422
  182.6 82.6 %collective-permute-start = (bf16[2,256,1408]{2,1,0:T(8,128)(2,1)}, bf16[2,256,1408]{2,1,0:T(8,128)(2,1)S(1)}, u32[]{:S(2)}, u32[]{:S(2)}) collective-permute-start(bf16[2,256,1408]{2,1,0:T(8,128)(2,1)} %get-tuple-element.24), channel_id=1, source_target_pairs={{0,1},{1,0},{2,3},{3,2},{4,5},{5,4},{6,7},{7,6},{8,9},{9,8},{10,11... | collective-permute-start | bytes 4325384 | tf_op jit(solution)/shard_map/ppermute | solution.py:422
  182.7 82.5 %collective-permute-start.1 = (bf16[2,256,1408]{2,1,0:T(8,128)(2,1)}, bf16[2,256,1408]{2,1,0:T(8,128)(2,1)S(1)}, u32[]{:S(2)}, u32[]{:S(2)}) collective-permute-start(bf16[2,256,1408]{2,1,0:T(8,128)(2,1)} %get-tuple-element.25), channel_id=1, source_target_pairs={{0,2},{1,3},{2,0},{3,1},{4,6},{5,7},{6,4},{7,5},{8,10},{9,11},{10,... | collective-permute-start | bytes 4325384 | tf_op jit(solution)/shard_map/ppermute | solution.py:422
  198.4 66.8 %collective-permute-start.2 = (bf16[2,256,1408]{2,1,0:T(8,128)(2,1)}, bf16[2,256,1408]{2,1,0:T(8,128)(2,1)}, u32[]{:S(2)}, u32[]{:S(2)}) collective-permute-start(bf16[2,256,1408]{2,1,0:T(8,128)(2,1)} %get-tuple-element.26), channel_id=1, source_target_pairs={{0,3},{1,2},{2,1},{3,0},{4,7},{5,6},{6,5},{7,4},{8,11},{9,10},{10,... | collective-permute-start | bytes 4325384 | tf_op jit(solution)/shard_map/ppermute | solution.py:422
  263.1 59.6 %collective-permute-start.9 = (bf16[2,256,1408]{2,1,0:T(8,128)(2,1)}, bf16[2,256,1408]{2,1,0:T(8,128)(2,1)}, u32[]{:S(2)}, u32[]{:S(2)}) collective-permute-start(bf16[2,256,1408]{2,1,0:T(8,128)(2,1)} %get-tuple-element.38), channel_id=1, source_target_pairs={{0,1},{1,0},{2,3},{3,2},{4,5},{5,4},{6,7},{7,6},{8,9},{9,8},{10,11... | collective-permute-start | bytes 4325384 | tf_op jit(solution)/shard_map/ppermute | solution.py:422
  263.3 59.6 %collective-permute-start.10 = (bf16[2,256,1408]{2,1,0:T(8,128)(2,1)}, bf16[2,256,1408]{2,1,0:T(8,128)(2,1)}, u32[]{:S(2)}, u32[]{:S(2)}) collective-permute-start(bf16[2,256,1408]{2,1,0:T(8,128)(2,1)} %get-tuple-element.39), channel_id=1, source_target_pairs={{0,2},{1,3},{2,0},{3,1},{4,6},{5,7},{6,4},{7,5},{8,10},{9,11},{10,... | collective-permute-start | bytes 4325384 | tf_op jit(solution)/shard_map/ppermute | solution.py:422
  265.2 1.2 copy-start
  265.2 62.9 %collective-permute-start.11 = (bf16[2,256,1408]{2,1,0:T(8,128)(2,1)}, bf16[2,256,1408]{2,1,0:T(8,128)(2,1)}, u32[]{:S(2)}, u32[]{:S(2)}) collective-permute-start(bf16[2,256,1408]{2,1,0:T(8,128)(2,1)} %get-tuple-element.40), channel_id=1, source_target_pairs={{0,3},{1,2},{2,1},{3,0},{4,7},{5,6},{6,5},{7,4},{8,11},{9,10},{10,... | collective-permute-start | bytes 4325384 | tf_op jit(solution)/shard_map/ppermute | solution.py:422
  265.2 1.6 copy-start.1
  321.0 133.7 %collective-permute-start.3 = (bf16[2,256,1408]{2,1,0:T(8,128)(2,1)}, bf16[2,256,1408]{2,1,0:T(8,128)(2,1)S(1)}, u32[]{:S(2)}, u32[]{:S(2)}) collective-permute-start(bf16[2,256,1408]{2,1,0:T(8,128)(2,1)} %get-tuple-element.28), channel_id=1, source_target_pairs={{0,1},{1,0},{2,3},{3,2},{4,5},{5,4},{6,7},{7,6},{8,9},{9,8},{10,11... | collective-permute-start | bytes 4325384 | tf_op jit(solution)/shard_map/ppermute | solution.py:422
  321.1 133.7 %collective-permute-start.4 = (bf16[2,256,1408]{2,1,0:T(8,128)(2,1)}, bf16[2,256,1408]{2,1,0:T(8,128)(2,1)S(1)}, u32[]{:S(2)}, u32[]{:S(2)}) collective-permute-start(bf16[2,256,1408]{2,1,0:T(8,128)(2,1)} %get-tuple-element.29), channel_id=1, source_target_pairs={{0,2},{1,3},{2,0},{3,1},{4,6},{5,7},{6,4},{7,5},{8,10},{9,11},{10,... | collective-permute-start | bytes 4325384 | tf_op jit(solution)/shard_map/ppermute | solution.py:422
  322.7 132.1 %collective-permute-start.5 = (bf16[2,256,1408]{2,1,0:T(8,128)(2,1)}, bf16[2,256,1408]{2,1,0:T(8,128)(2,1)}, u32[]{:S(2)}, u32[]{:S(2)}) collective-permute-start(bf16[2,256,1408]{2,1,0:T(8,128)(2,1)} %get-tuple-element.30), channel_id=1, source_target_pairs={{0,3},{1,2},{2,1},{3,0},{4,7},{5,6},{6,5},{7,4},{8,11},{9,10},{10,... | collective-permute-start | bytes 4325384 | tf_op jit(solution)/shard_map/ppermute | solution.py:422
  454.7 1.1 copy-start.2
  454.8 1.6 copy-start.3

commit v4 on v3

--- a/solution.py
+++ b/solution.py
@@ -9,7 +9,7 @@
 
 LN_EPS = 1e-6
 LOG2E = 1.4426950408889634
-VMEM_LIMIT = 60 * 1024 * 1024
+VMEM_LIMIT = 67043328
 NT = (((1,), (1,)), ((), ()))
 TN = (((0,), (0,)), ((), ()))
 F32 = jnp.float32
@@ -161,7 +161,7 @@
             dst[:, :, tokens] = part.reshape(heads, dim, 2 * quarter).astype(BF16)
 
     def attend(srcs, index):
-        for i in range(heads // 2):
+        def pair(i, carry):
             rows = pl.ds(pl.multiple_of(index * group + 2 * i * dim, 2 * dim), 2 * dim)
             for cols in range(0, quarter, 128):
                 first = attend_frames(*srcs, 2 * i, cols, quarter, scale)
@@ -169,6 +169,9 @@
                 for t in range(4):
                     out = jnp.concatenate([first[t], second[t]], axis=0)
                     a_s[rows, t * quarter + cols:t * quarter + cols + 128] = out.astype(BF16)
+            return carry
+
+        lax.fori_loop(0, heads // 2, pair, 0)
 
     halves = (slice(0, 2 * quarter), slice(2 * quarter, 4 * quarter))
     first, second = (qa, ka, va), (qb, kb, vb)
@@ -177,18 +180,12 @@
     def _():
         for d in range(4):
             shift(d)
-        for tokens in halves:
-            project(0, first, tokens)
-
-    @pl.when(g > 0)
-    def _():
-        for tokens in halves:
-            project(0, first, tokens)
-        attend(second, 2 * g - 1)
 
     for tokens in halves:
+        project(0, first, tokens)
         project(1, second, tokens)
     attend(first, 2 * g)
+    attend(second, 2 * g + 1)
 
     @pl.when((v == 0) & (g == 0))
     def _():
@@ -200,7 +197,6 @@
 
     @pl.when(g == pl.num_programs(1) - 1)
     def _():
-        attend(second, 2 * g + 1)
         for d, (x, o_ref) in enumerate(zip(frames, (o0, o1, o2, o3))):
             branch = dot(a_s[:, d * quarter:(d + 1) * quarter], wo_s[...], TN)
             o_ref[...] = (x[...].astype(F32) + mod_ref[2:3, :] * branch).astype(BF16)
@@ -345,37 +341,37 @@
     )(me, *frames, modulation, pos, w_qkv.reshape(3, total, width), w_out.reshape(total, width))
 
 
-def text_kv(text, w_kv, heads):
+def text_kv(text, w_kv, heads, part, parts):
     videos, length, width = text.shape
     dim = w_kv.shape[2]
     count = w_kv.shape[1]
     total = count * dim
-    tokens = videos * length
+    tokens = videos * length // parts
     return pl.pallas_call(
         functools.partial(text_kernel, heads=heads, dim=dim),
         grid=(count // heads,),
-        in_specs=[resident((tokens, width)), pl.BlockSpec((2, heads * dim, width), lambda g: (0, g, 0))],
+        in_specs=[pl.BlockSpec((tokens, width), lambda g: (part, 0), pipeline_mode=pl.Buffered(1)), pl.BlockSpec((2, heads * dim, width), lambda g: (0, g, 0))],
         out_specs=[pl.BlockSpec((heads, tokens, 128), lambda g: (g, 0, 0)), pl.BlockSpec((heads, dim, tokens), lambda g: (g, 0, 0))],
         out_shape=[jax.ShapeDtypeStruct((count, tokens, 128), BF16), jax.ShapeDtypeStruct((count, dim, tokens), BF16)],
         compiler_params=params(1),
         cost_estimate=cost(4 * tokens * width * total, 2 * (2 * total * width + 3 * tokens * width)),
         name="text_kv",
-    )(text.reshape(tokens, width), w_kv.reshape(2, total, width))
+    )(text.reshape(videos * length, width), w_kv.reshape(2, total, width))
 
 
 def cross_mlp(me, chunks, modulation, k, v_t, w_query, w_out_cross, w_in, w_out, base, y, videos):
     count, quarter, width = chunks[0].shape
     tokens = 4 * quarter
     heads, dim, all_text = v_t.shape
-    text = all_text // videos
+    text = all_text // count
     total = heads * dim
     hidden = w_in.shape[1]
     tile = 512
     steps = hidden // tile
     in_specs = [pl.BlockSpec((None, quarter, width), lambda v, s, me: (v, 0, 0))] * 4 + [
         pl.BlockSpec((None, 6, width), lambda v, s, me: (base + v, 0, 0)),
-        pl.BlockSpec((heads, text, k.shape[2]), lambda v, s, me: (0, base + v, 0)),
-        pl.BlockSpec((heads, dim, text), lambda v, s, me: (0, 0, base + v)),
+        pl.BlockSpec((heads, text, k.shape[2]), lambda v, s, me: (0, v, 0)),
+        pl.BlockSpec((heads, dim, text), lambda v, s, me: (0, 0, v)),
         pl.BlockSpec(memory_space=pl.ANY),
         pl.BlockSpec(memory_space=pl.ANY),
         pl.BlockSpec((width, tile), lambda v, s, me: (0, s)),
@@ -436,11 +432,17 @@
         me = lax.axis_index('sp').astype(jnp.int32).reshape(1)
         bases = range(0, videos, 2)
         by_patch = [swap(spatial(me, latents, modulation, w_qkv_spatial, w_out_spatial, b, 2, 4), devices) for b in bases]
-        k, v_t = text_kv(text_ctx, w_kv_cross, 4)
-        by_frame = [swap(temporal(me, by_patch[i], modulation, pos_temporal, w_qkv_temporal, w_out_temporal, b, 4), devices) for i, b in enumerate(bases)]
+        text, _ = lax.optimization_barrier((text_ctx, by_patch[-1][0]))
+        context = [text_kv(text, w_kv_cross, 4, 0, 2)]
+        first, _ = lax.optimization_barrier((by_patch[0], context[0][1]))
+        by_patch = [first] + by_patch[1:]
+        mixed = [temporal(me, by_patch[i], modulation, pos_temporal, w_qkv_temporal, w_out_temporal, b, 4) for i, b in enumerate(bases)]
+        by_frame = [swap(parts, devices) for parts in mixed]
+        text, _ = lax.optimization_barrier((text_ctx, mixed[-1][0]))
+        context.append(text_kv(text, w_kv_cross, 4, 1, 2))
         y = None
         for i, b in enumerate(bases):
-            y = cross_mlp(me, by_frame[i], modulation, k, v_t, w_query_cross, w_out_cross, w_mlp_in, w_mlp_out, b, y, videos)
+            y = cross_mlp(me, by_frame[i], modulation, *context[i], w_query_cross, w_out_cross, w_mlp_in, w_mlp_out, b, y, videos)
         return y
 
     return jax.shard_map(local_block, mesh=mesh, in_specs=in_specs, out_specs=act_spec, check_vma=False)

time: 594 us -> 579 us (0.975)
  Pallas kernels: 564 us -> 557 us
    pallas_call x2, Pallas kernels: 119 us -> 108 us  [temporal(): pl.pallas_call(functools.partial(temporal_kernel, heads=heads, dim=dim),...]
    pallas_call x1 -> x2, Pallas kernels: 13.8 us -> 17.6 us  [text_kv(): pl.pallas_call(functools.partial(text_kernel, heads=heads, dim=dim), grid...]
  transfers between devices with their start and end apart: 12 -> 12, of which waited for: 1 -> 0; matrix products, arithmetic and copies ran while one was open for 0% -> 0% of each run, Pallas kernels for 60% -> 60%
where the time goes in v4:
time: 579 us; the launch traced here: 569 us
  Pallas kernels  557 us (96%)
  starting transfers between devices  9.76 us (2%)
    pallas_call x2, Pallas kernels, cross_mlp(): pl.pallas_call(functools.partial(cross_mlp_kernel, heads=heads, dim=dim),...  254 us
    pallas_call x2, Pallas kernels, spatial(): pl.pallas_call(functools.partial(spatial_kernel, heads=heads, dim=dim), g...  178 us
    pallas_call x2, Pallas kernels, temporal(): pl.pallas_call(functools.partial(temporal_kernel, heads=heads, dim=dim),...  108 us
    pallas_call x2, Pallas kernels, text_kv(): pl.pallas_call(functools.partial(text_kernel, heads=heads, dim=dim), grid...  17.6 us
  transfers between devices with their start and end apart: 12, of which 0 were waited for; matrix products, arithmetic and copies ran while one was open for 0% of the time, Pallas kernels for 60%

profile of v4, /device:TPU:0, one launch (start us, length us, event | category | flops | bytes accessed | tf_op | source)
XLA Modules:
  0.0 569.2 jit_solution(1785660071611054967)
XLA Ops:
  0.0 1.6 copy.15.mod_ref
  1.6 88.6 %spatial.3 = (bf16[2,256,1408]{2,1,0:T(8,128)(2,1)}, bf16[2,256,1408]{2,1,0:T(8,128)(2,1)}, bf16[2,256,1408]{2,1,0:T(8,128)(2,1)}, bf16[2,256,1408]{2,1,0:T(8,128)(2,1)}) custom-call(s32[1]{0:T(128)} %bitcast.me_ref, bf16[4,1,1024,1408]{3,2,1,0:T(8,128)(2,1)} %x_ref.3, f32[4,6,1408]{2,1,0:T(8,128)} %copy.15.mod_ref, bf16[3,1408,1408]{2,1,0:T(8,128)(2,1)} %bitcast.10, ...), custom_call_target="tpu_custom_call" | custom-call | flops 44291850240 | bytes 27394048 | tf_op jit(solution)/shard_map/spatial/pallas_call | solution.py:302
  90.2 0.8 collective-permute-start.6
  91.0 2.5 collective-permute-start.7
  93.5 0.1 collective-permute-start.8
  93.6 89.2 %spatial.2 = (bf16[2,256,1408]{2,1,0:T(8,128)(2,1)}, bf16[2,256,1408]{2,1,0:T(8,128)(2,1)}, bf16[2,256,1408]{2,1,0:T(8,128)(2,1)}, bf16[2,256,1408]{2,1,0:T(8,128)(2,1)}) custom-call(s32[1]{0:T(128)} %bitcast.me_ref, bf16[4,1,1024,1408]{3,2,1,0:T(8,128)(2,1)} %x_ref.3, f32[4,6,1408]{2,1,0:T(8,128)} %copy.15.mod_ref, bf16[3,1408,1408]{2,1,0:T(8,128)(2,1)} %bitcast.11, ...), custom_call_target="tpu_custom_call" | custom-call | flops 44291850240 | bytes 27394048 | tf_op jit(solution)/shard_map/spatial/pallas_call | solution.py:302
  182.8 0.2 collective-permute-start
  182.9 1.9 collective-permute-start.1
  184.9 8.8 %text_kv.3 = (bf16[16,512,128]{2,1,0:T(8,128)(2,1)}, bf16[16,88,512]{2,1,0:T(8,128)(2,1)}) custom-call(bf16[1024,1408]{1,0:T(8,128)(2,1)} %bitcast.24, bf16[2,1408,1408]{2,1,0:T(8,128)(2,1)} %bitcast.14), custom_call_target="tpu_custom_call" | custom-call | flops 4060086272 | bytes 12255232 | tf_op jit(solution)/shard_map/text_kv/pallas_call | solution.py:350
  193.6 0.0 collective-permute-done.6.x1
  193.6 0.0 collective-permute-start.2
  193.7 0.0 collective-permute-done.7.x2
  193.7 0.0 collective-permute-done.8.x3
  193.7 54.1 %temporal.3 = (bf16[2,256,1408]{2,1,0:T(8,128)(2,1)}, bf16[2,256,1408]{2,1,0:T(8,128)(2,1)}, bf16[2,256,1408]{2,1,0:T(8,128)(2,1)}, bf16[2,256,1408]{2,1,0:T(8,128)(2,1)}) custom-call(s32[1]{0:T(128)} %bitcast.me_ref, bf16[2,256,1408]{2,1,0:T(8,128)(2,1)} %get-tuple-element.48.x0, bf16[2,256,1408]{2,1,0:T(8,128)(2,1)} %collective-permute-done.6.x1, ...), custom_call_target="tpu_custom_call" | custom-call | flops 32480690176 | bytes 27394048 | tf_op jit(solution)/shard_map/temporal/pallas_call | solution.py:334
  247.8 0.2 collective-permute-start.9
  248.0 1.9 collective-permute-start.10
  250.0 0.0 collective-permute-done.x1
  250.0 0.0 collective-permute-start.11
  250.0 0.0 collective-permute-done.1.x2
  250.0 0.0 collective-permute-done.2.x3
  250.0 53.7 %temporal.2 = (bf16[2,256,1408]{2,1,0:T(8,128)(2,1)}, bf16[2,256,1408]{2,1,0:T(8,128)(2,1)}, bf16[2,256,1408]{2,1,0:T(8,128)(2,1)}, bf16[2,256,1408]{2,1,0:T(8,128)(2,1)}) custom-call(s32[1]{0:T(128)} %bitcast.me_ref, bf16[2,256,1408]{2,1,0:T(8,128)(2,1)} %get-tuple-element.31.x0, bf16[2,256,1408]{2,1,0:T(8,128)(2,1)} %collective-permute-done.x1, ...), custom_call_target="tpu_custom_call" | custom-call | flops 32480690176 | bytes 27394048 | tf_op jit(solution)/shard_map/temporal/pallas_call | solution.py:334
  303.7 0.2 collective-permute-start.3
  304.0 1.9 collective-permute-start.4
  305.9 8.8 %text_kv.2 = (bf16[16,512,128]{2,1,0:T(8,128)(2,1)}, bf16[16,88,512]{2,1,0:T(8,128)(2,1)}) custom-call(bf16[1024,1408]{1,0:T(8,128)(2,1)} %bitcast.25, bf16[2,1408,1408]{2,1,0:T(8,128)(2,1)} %bitcast.15), custom_call_target="tpu_custom_call" | custom-call | flops 4060086272 | bytes 12255232 | tf_op jit(solution)/shard_map/text_kv/pallas_call | solution.py:350
  314.7 0.0 collective-permute-done.9.x1
  314.7 0.0 collective-permute-start.5
  314.7 0.0 collective-permute-done.10.x2
  314.8 0.0 collective-permute-done.11.x3
  314.8 126.8 %cross_mlp.2.rest_0_ = bf16[4,1,1024,1408]{3,2,1,0:T(8,128)(2,1)} custom-call(s32[1]{0:T(128)} %bitcast.me_ref, bf16[2,256,1408]{2,1,0:T(8,128)(2,1)} %get-tuple-element.52.x0, bf16[2,256,1408]{2,1,0:T(8,128)(2,1)} %collective-permute-done.9.x1, bf16[2,256,1408]{2,1,0:T(8,128)(2,1)} %collective-permute-done.10.x2, ...), custom_call_target="tpu_custom_call" | custom-call | flops 82678120448 | bytes 45416448 | tf_op jit(solution)/shard_map/cross_mlp/pallas_call | solution.py:406
  441.6 0.0 collective-permute-done.3.x1
  441.6 0.0 collective-permute-done.4.x2
  441.6 0.0 collective-permute-done.5.x3
  441.6 127.2 %cross_mlp.3 = bf16[4,1,1024,1408]{3,2,1,0:T(8,128)(2,1)} custom-call(s32[1]{0:T(128)} %bitcast.me_ref, bf16[2,256,1408]{2,1,0:T(8,128)(2,1)} %get-tuple-element.35.x0, bf16[2,256,1408]{2,1,0:T(8,128)(2,1)} %collective-permute-done.3.x1, bf16[2,256,1408]{2,1,0:T(8,128)(2,1)} %collective-permute-done.4.x2, ...), custom_call_target="tpu_custom_call", output_to_operand_aliasing={{}: (12, {})} | custom-call | flops 82678120448 | bytes 45416448 | tf_op jit(solution)/shard_map/cross_mlp/pallas_call | solution.py:406
Async XLA Ops:
  90.2 103.4 %collective-permute-start.6 = (bf16[2,256,1408]{2,1,0:T(8,128)(2,1)}, bf16[2,256,1408]{2,1,0:T(8,128)(2,1)}, u32[]{:S(2)}, u32[]{:S(2)}) collective-permute-start(bf16[2,256,1408]{2,1,0:T(8,128)(2,1)} %get-tuple-element.43), channel_id=1, source_target_pairs={{0,1},{1,0},{2,3},{3,2},{4,5},{5,4},{6,7},{7,6},{8,9},{9,8},{10,11... | collective-permute-start | bytes 4325384 | tf_op jit(solution)/shard_map/ppermute | solution.py:418
  91.0 102.7 %collective-permute-start.7 = (bf16[2,256,1408]{2,1,0:T(8,128)(2,1)}, bf16[2,256,1408]{2,1,0:T(8,128)(2,1)}, u32[]{:S(2)}, u32[]{:S(2)}) collective-permute-start(bf16[2,256,1408]{2,1,0:T(8,128)(2,1)} %get-tuple-element.44), channel_id=1, source_target_pairs={{0,2},{1,3},{2,0},{3,1},{4,6},{5,7},{6,4},{7,5},{8,10},{9,11},{10,... | collective-permute-start | bytes 4325384 | tf_op jit(solution)/shard_map/ppermute | solution.py:418
  93.5 100.2 %collective-permute-start.8 = (bf16[2,256,1408]{2,1,0:T(8,128)(2,1)}, bf16[2,256,1408]{2,1,0:T(8,128)(2,1)}, u32[]{:S(2)}, u32[]{:S(2)}) collective-permute-start(bf16[2,256,1408]{2,1,0:T(8,128)(2,1)} %get-tuple-element.45), channel_id=1, source_target_pairs={{0,3},{1,2},{2,1},{3,0},{4,7},{5,6},{6,5},{7,4},{8,11},{9,10},{10,... | collective-permute-start | bytes 4325384 | tf_op jit(solution)/shard_map/ppermute | solution.py:418
  182.8 67.2 %collective-permute-start = (bf16[2,256,1408]{2,1,0:T(8,128)(2,1)}, bf16[2,256,1408]{2,1,0:T(8,128)(2,1)}, u32[]{:S(2)}, u32[]{:S(2)}) collective-permute-start(bf16[2,256,1408]{2,1,0:T(8,128)(2,1)} %get-tuple-element.32), channel_id=1, source_target_pairs={{0,1},{1,0},{2,3},{3,2},{4,5},{5,4},{6,7},{7,6},{8,9},{9,8},{10,11... | collective-permute-start | bytes 4325384 | tf_op jit(solution)/shard_map/ppermute | solution.py:418
  182.9 67.0 %collective-permute-start.1 = (bf16[2,256,1408]{2,1,0:T(8,128)(2,1)}, bf16[2,256,1408]{2,1,0:T(8,128)(2,1)}, u32[]{:S(2)}, u32[]{:S(2)}) collective-permute-start(bf16[2,256,1408]{2,1,0:T(8,128)(2,1)} %get-tuple-element.33), channel_id=1, source_target_pairs={{0,2},{1,3},{2,0},{3,1},{4,6},{5,7},{6,4},{7,5},{8,10},{9,11},{10,... | collective-permute-start | bytes 4325384 | tf_op jit(solution)/shard_map/ppermute | solution.py:418
  193.6 56.3 %collective-permute-start.2 = (bf16[2,256,1408]{2,1,0:T(8,128)(2,1)}, bf16[2,256,1408]{2,1,0:T(8,128)(2,1)}, u32[]{:S(2)}, u32[]{:S(2)}) collective-permute-start(bf16[2,256,1408]{2,1,0:T(8,128)(2,1)} %get-tuple-element.34), channel_id=1, source_target_pairs={{0,3},{1,2},{2,1},{3,0},{4,7},{5,6},{6,5},{7,4},{8,11},{9,10},{10,... | collective-permute-start | bytes 4325384 | tf_op jit(solution)/shard_map/ppermute | solution.py:418
  247.8 66.9 %collective-permute-start.9 = (bf16[2,256,1408]{2,1,0:T(8,128)(2,1)}, bf16[2,256,1408]{2,1,0:T(8,128)(2,1)}, u32[]{:S(2)}, u32[]{:S(2)}) collective-permute-start(bf16[2,256,1408]{2,1,0:T(8,128)(2,1)} %get-tuple-element.53), channel_id=1, source_target_pairs={{0,1},{1,0},{2,3},{3,2},{4,5},{5,4},{6,7},{7,6},{8,9},{9,8},{10,11... | collective-permute-start | bytes 4325384 | tf_op jit(solution)/shard_map/ppermute | solution.py:418
  248.0 66.7 %collective-permute-start.10 = (bf16[2,256,1408]{2,1,0:T(8,128)(2,1)}, bf16[2,256,1408]{2,1,0:T(8,128)(2,1)}, u32[]{:S(2)}, u32[]{:S(2)}) collective-permute-start(bf16[2,256,1408]{2,1,0:T(8,128)(2,1)} %get-tuple-element.54), channel_id=1, source_target_pairs={{0,2},{1,3},{2,0},{3,1},{4,6},{5,7},{6,4},{7,5},{8,10},{9,11},{10,... | collective-permute-start | bytes 4325384 | tf_op jit(solution)/shard_map/ppermute | solution.py:418
  250.0 64.8 %collective-permute-start.11 = (bf16[2,256,1408]{2,1,0:T(8,128)(2,1)}, bf16[2,256,1408]{2,1,0:T(8,128)(2,1)}, u32[]{:S(2)}, u32[]{:S(2)}) collective-permute-start(bf16[2,256,1408]{2,1,0:T(8,128)(2,1)} %get-tuple-element.55), channel_id=1, source_target_pairs={{0,3},{1,2},{2,1},{3,0},{4,7},{5,6},{6,5},{7,4},{8,11},{9,10},{10,... | collective-permute-start | bytes 4325384 | tf_op jit(solution)/shard_map/ppermute | solution.py:418
  303.7 137.8 %collective-permute-start.3 = (bf16[2,256,1408]{2,1,0:T(8,128)(2,1)}, bf16[2,256,1408]{2,1,0:T(8,128)(2,1)}, u32[]{:S(2)}, u32[]{:S(2)}) collective-permute-start(bf16[2,256,1408]{2,1,0:T(8,128)(2,1)} %get-tuple-element.36), channel_id=1, source_target_pairs={{0,1},{1,0},{2,3},{3,2},{4,5},{5,4},{6,7},{7,6},{8,9},{9,8},{10,11... | collective-permute-start | bytes 4325384 | tf_op jit(solution)/shard_map/ppermute | solution.py:418
  304.0 137.6 %collective-permute-start.4 = (bf16[2,256,1408]{2,1,0:T(8,128)(2,1)}, bf16[2,256,1408]{2,1,0:T(8,128)(2,1)}, u32[]{:S(2)}, u32[]{:S(2)}) collective-permute-start(bf16[2,256,1408]{2,1,0:T(8,128)(2,1)} %get-tuple-element.37), channel_id=1, source_target_pairs={{0,2},{1,3},{2,0},{3,1},{4,6},{5,7},{6,4},{7,5},{8,10},{9,11},{10,... | collective-permute-start | bytes 4325384 | tf_op jit(solution)/shard_map/ppermute | solution.py:418
  314.7 126.8 %collective-permute-start.5 = (bf16[2,256,1408]{2,1,0:T(8,128)(2,1)}, bf16[2,256,1408]{2,1,0:T(8,128)(2,1)}, u32[]{:S(2)}, u32[]{:S(2)}) collective-permute-start(bf16[2,256,1408]{2,1,0:T(8,128)(2,1)} %get-tuple-element.38), channel_id=1, source_target_pairs={{0,3},{1,2},{2,1},{3,0},{4,7},{5,6},{6,5},{7,4},{8,11},{9,10},{10,... | collective-permute-start | bytes 4325384 | tf_op jit(solution)/shard_map/ppermute | solution.py:418
